TPU v7x, 256 devices: a whole 4x4x8 slice. The times are simulated.
256 devices in a mesh: group: 32 (over x_hi, z, core), tensor: 8 (over y, x_lo).
Axes of the slice: x: 4 (x_hi: 2, x_lo: 2; x = x_hi * 2 + x_lo), y: 4, z: 8, core: 2. Of those that a mesh axis runs over, the one named last changes fastest.
Arguments:
- hidden: bfloat16 [64, 16384], P('group'), may hold values from -6 to 6
- norm_gain: float32 [16384], replicated, may hold values from 0.1 to 1.9
- slab_of: int32 [32], replicated, may hold values from 0 to 31, each once
- w_query: bfloat16 [16384, 16384], P('group', 'tensor'), may hold values from -0.046875 to 0.046875
- w_key: bfloat16 [16384, 1024], P('group', 'tensor'), may hold values from -0.046875 to 0.046875
- w_value: bfloat16 [16384, 1024], P('group', 'tensor'), may hold values from -0.046875 to 0.046875
- w_out: bfloat16 [16384, 16384], P('tensor', 'group'), may hold values from -0.046875 to 0.046875
- k_cache: bfloat16 [64, 8, 4096, 128], P('group', 'tensor'), may hold values from -1000 to 1000
- v_cache: bfloat16 [64, 8, 4096, 128], P('group', 'tensor'), may hold values from -6 to 6
- lengths: int32 [64], P('group'), may hold values from 1 to 4096, as said below
Outputs:
- out_hidden: bfloat16 [64, 16384], P('group')
- new_keys: bfloat16 [64, 8, 128], P('group', 'tensor')
- new_values: bfloat16 [64, 8, 128], P('group', 'tensor')
Inputs may be any that keep to these rules, and one draw needn't show every extreme that they name: `lengths`: some sequence holds exactly 4096 cached positions.
All inputs are finite; a program needn't handle non-finite values.
Results may differ from a plain program's by a relative error of at most 0.0085.
Values may be sent and summed in bfloat16 or wider, within the bound.
No kernel may reach another device: no remote copies, remote signals or barrier semaphores. Data moves between devices by JAX's collectives and lax.ppermute only.
A program may use at most 64 MiB of HBM per device.

v0:
```python
import math

import jax
import jax.numpy as jnp
from jax import lax
from jax.sharding import PartitionSpec as P


def cut_along(shard, dim, size):
    before, after = (shard.shape[:dim], shard.shape[dim + 1 :])
    return jnp.moveaxis(shard.reshape(*before, size, -1, *after), dim, 0)


def summed_on_arrival(shard, axis, dim):
    tiles = cut_along(shard, dim, lax.axis_size(axis))
    arrived = lax.all_to_all(tiles, axis, split_axis=0, concat_axis=0, tiled=True)
    return arrived.sum(axis=0)


def sent_to_all(shard, axis):
    size = lax.axis_size(axis)
    return lax.all_to_all(
        jnp.broadcast_to(shard[None], (size, *shard.shape)), axis, 0, 0, tiled=True
    )


def in_order(tiles, dim):
    shape = list(tiles.shape[1:])
    shape[dim] *= tiles.shape[0]
    return jnp.moveaxis(tiles, 0, dim).reshape(shape)


def collect(shard, axis, dim):
    tiles = sent_to_all(shard, axis)
    return in_order(tiles, dim)


def of_everyone(shard, axis):
    everything = sent_to_all(shard, axis)
    return jnp.sum(everything.astype(jnp.float32), axis=0)


def rotate(values, angles):
    half_dim = values.shape[-1] // 2
    cosine = jnp.cos(angles)
    sine_part = jnp.sin(angles)
    first_half = values[..., :half_dim]
    second_half = values[..., half_dim:]
    return jnp.concatenate(
        [
            first_half * cosine - second_half * sine_part,
            second_half * cosine + first_half * sine_part,
        ],
        axis=-1,
    )


def angles_for(lengths, head_dim):
    half_dim = head_dim // 2
    frequency = jnp.exp(
        -math.log(500000.0) * (2.0 * jnp.arange(half_dim, dtype=jnp.float32)) / head_dim
    )
    return lengths.astype(jnp.float32)[:, None] * frequency[None, :]


def body(hidden, norm_gain, slab_of, w_query, w_key, w_value, w_out, k_cache, v_cache, lengths):
    groups = lax.axis_size("group")
    sequences, model_width = hidden.shape
    slab_width = model_width // groups
    hidden_wide = hidden.astype(jnp.float32)
    mean_square = jnp.mean(hidden_wide * hidden_wide, axis=1, keepdims=True)
    normed = (hidden_wide * lax.rsqrt(mean_square + 1e-05) * norm_gain).astype(jnp.bfloat16)
    arranged = jnp.take(normed.reshape(sequences, groups, slab_width), slab_of, axis=1).reshape(
        sequences, model_width
    )
    own_columns = lax.all_to_all(arranged, "group", split_axis=1, concat_axis=0, tiled=True)
    projected = summed_on_arrival(
        jnp.concatenate(
            [
                jnp.dot(own_columns, w_query, preferred_element_type=jnp.float32),
                jnp.dot(own_columns, w_key, preferred_element_type=jnp.float32),
                jnp.dot(own_columns, w_value, preferred_element_type=jnp.float32),
            ],
            axis=1,
        ),
        "group",
        0,
    )
    head_dim = k_cache.shape[3]
    kv_local = k_cache.shape[1]
    query_cols = w_query.shape[1]
    key_cols = w_key.shape[1]
    queries = projected[:, :query_cols].reshape(sequences, query_cols // head_dim, head_dim)
    keys_new = projected[:, query_cols : query_cols + key_cols].reshape(
        sequences, kv_local, head_dim
    )
    values_new = projected[:, query_cols + key_cols :].reshape(sequences, kv_local, head_dim)
    angles = angles_for(lengths, head_dim)[:, None, :]
    new_keys = rotate(keys_new, angles).astype(jnp.bfloat16)
    new_values = values_new.astype(jnp.bfloat16)
    group_ratio = queries.shape[1] // kv_local
    scaled = (
        (rotate(queries, angles) / math.sqrt(head_dim))
        .astype(jnp.bfloat16)
        .reshape(sequences, kv_local, group_ratio, head_dim)
    )
    scores = jnp.einsum("bgrd,bgld->bgrl", scaled, k_cache, preferred_element_type=jnp.float32)
    own_score = jnp.einsum("bgrd,bgd->bgr", scaled, new_keys, preferred_element_type=jnp.float32)
    visible = (jnp.arange(k_cache.shape[2])[None, :] < lengths[:, None])[:, None, None, :]
    masked = jnp.where(visible, scores, -1e30)
    highest = jnp.maximum(jnp.max(masked, axis=-1), own_score)
    exponent = jnp.where(visible, jnp.exp(masked - highest[..., None]), 0.0)
    own_exp = jnp.exp(own_score - highest)
    denominator = jnp.sum(exponent, axis=-1) + own_exp
    weights = (exponent / denominator[..., None]).astype(jnp.bfloat16)
    own_weight = (own_exp / denominator).astype(jnp.bfloat16)
    combined = jnp.einsum("bgrl,bgld->bgrd", weights, v_cache, preferred_element_type=jnp.float32)
    combined = (
        combined
        + own_weight.astype(jnp.float32)[..., None] * new_values.astype(jnp.float32)[:, :, None, :]
    )
    attended = combined.astype(jnp.bfloat16).reshape(sequences, query_cols)
    head_partial = jnp.dot(collect(attended, "group", 0), w_out, preferred_element_type=jnp.float32)
    inverse = jnp.argsort(slab_of)
    summed = of_everyone(head_partial.astype(jnp.bfloat16), "tensor").astype(jnp.float32)
    returned = (
        lax.all_to_all(
            summed.astype(jnp.bfloat16), "group", split_axis=0, concat_axis=1, tiled=True
        )
        .astype(summed.dtype)
        .reshape(sequences, groups, slab_width)
    )
    ordered = jnp.take(returned, inverse, axis=1).reshape(sequences, model_width)
    out_hidden = (hidden_wide + ordered).astype(jnp.bfloat16)
    return (out_hidden, new_keys, new_values)


def solution(mesh):
    in_specs = (
        P("group", None),
        P(),
        P(),
        P("group", "tensor"),
        P("group", "tensor"),
        P("group", "tensor"),
        P("tensor", "group"),
        P("group", "tensor", None, None),
        P("group", "tensor", None, None),
        P("group"),
    )
    out_specs = (P("group", None), P("group", "tensor", None), P("group", "tensor", None))
    return jax.shard_map(body, mesh=mesh, in_specs=in_specs, out_specs=out_specs, check_vma=False)
```

profile of v0, /device:TPU:2, one launch (start us, length us, event | category | flops | bytes accessed | tf_op | source)
XLA Modules:
  0.0 110.2 jit_solution(5413616316966951642)
XLA Ops:
  0.7 0.8 compare_select_fusion
  1.5 0.7 compare_and_fusion
  2.1 1.1 fusion.17
  3.2 1.0 fusion.19
  4.3 0.7 gather_fusion
  5.0 0.1 fusion.21
  5.1 20.8 %all_to_all.44 = bf16[2,32,512]{2,0,1:T(2,128)(2,1)S(1)} all-to-all(bf16[2,32,512]{2,0,1:T(2,128)(2,1)S(1)} %fusion.21), channel_id=1, replica_groups=mesh['group'=32,'tensor'=8] {'group'}, dimensions={1} | all-to-all | bytes 131072 | tf_op jit(solution)/shard_map/all_to_all | solution.py:76
  25.9 2.1 %fusion.39 = f32[64,2048]{1,0:T(8,128)S(1)} fusion(bf16[64,512]{1,0:T(8,128)(2,1)S(1)} %all_to_all.33, bf16[512,2048]{1,0:T(8,128)(2,1)} %param.13), kind=kOutput, calls=%fused_computation.71 | convolution fusion | flops 134217728 | bytes 2686976 | tf_op jit(solution)/shard_map/dot_general | solution.py:80
  28.0 0.2 fusion.40
  28.2 0.2 fusion.41
  28.4 1.2 %reshape.278 = f32[32,2,2304]{2,1,0:T(2,128)} reshape(f32[64,2304]{1,0:T(8,128)S(1)} %pad_maximum_fusion) | data formatting | bytes 1179648 | tf_op jit(solution)/shard_map/reshape | solution.py:11
  29.5 3.9 %all-to-all-start.1 = ((f32[32,2,2304]{2,1,0:T(2,128)}), f32[32,2,2304]{2,1,0:T(2,128)S(1)}, u32[]{:S(2)}, u32[]{:S(2)}) async-start(f32[32,2,2304]{2,1,0:T(2,128)} %reshape.278), calls=%async_computation.1 | async-start | bytes 1179648 | tf_op jit(solution)/shard_map/all_to_all | solution.py:16
  33.7 20.8 %all-to-all-done.1 = f32[32,2,2304]{2,1,0:T(2,128)S(1)} async-done(((f32[32,2,2304]{2,1,0:T(2,128)}), f32[32,2,2304]{2,1,0:T(2,128)S(1)}, u32[]{:S(2)}, u32[]{:S(2)}) %all-to-all-start.1) | async-done | bytes 589856 | tf_op jit(solution)/shard_map/all_to_all | solution.py:16
  54.5 0.2 reduce_sum.40
  54.7 0.5 fusion.36
  55.7 0.7 fusion.38
  56.4 0.3 fusion.12
  56.8 0.5 fusion.9
  57.2 0.8 broadcast_in_dim.81
  58.1 3.9 %all-to-all-start.2 = ((bf16[32,2,2048]{2,1,0:T(2,128)(2,1)}), bf16[32,2,2048]{2,1,0:T(2,128)(2,1)S(1)}, u32[]{:S(2)}, u32[]{:S(2)}) async-start(bf16[32,2,2048]{2,1,0:T(2,128)(2,1)} %broadcast_in_dim.81), calls=%async_computation.2 | async-start | bytes 524288 | tf_op jit(solution)/shard_map/all_to_all | solution.py:22
  62.0 1.6 %sort.17 = (s32[32]{0:T(128)}, s32[32]{0:T(128)S(1)}) sort(s32[32]{0:T(128)S(1)} %copy-done.6, s32[32]{0:T(128)S(1)} %iota.18), dimensions={0}, to_apply=%region_0.0 | sort | flops 160 | bytes 512 | tf_op jit(solution)/shard_map/jit(argsort)/sort | solution.py:124
  63.6 13.0 %all-to-all-done.2 = bf16[32,2,2048]{2,1,0:T(2,128)(2,1)S(1)} async-done(((bf16[32,2,2048]{2,1,0:T(2,128)(2,1)}), bf16[32,2,2048]{2,1,0:T(2,128)(2,1)S(1)}, u32[]{:S(2)}, u32[]{:S(2)}) %all-to-all-start.2) | async-done | bytes 262176 | tf_op jit(solution)/shard_map/all_to_all | solution.py:22
  76.7 2.1 %convolution_convert_fusion = bf16[64,512]{1,0:T(8,128)(2,1)S(1)} fusion(bf16[64,2048]{1,0:T(8,128)(2,1)S(1)} %reshape.283, bf16[2048,512]{1,0:T(8,128)(2,1)} %param.16), kind=kOutput, calls=%fused_computation.6 | convolution fusion | flops 134250496 | bytes 2424832 | tf_op jit(solution)/shard_map/dot_general | solution.py:123
  78.8 0.8 broadcast_in_dim.82
  79.6 5.9 %all-to-all-start.3 = ((bf16[8,64,512]{2,1,0:T(8,128)(2,1)}), bf16[8,64,512]{2,1,0:T(8,128)(2,1)S(1)}, u32[]{:S(2)}, u32[]{:S(2)}) async-start(bf16[8,64,512]{2,1,0:T(8,128)(2,1)} %broadcast_in_dim.82), calls=%async_computation.3 | async-start | bytes 1048576 | tf_op jit(solution)/shard_map/all_to_all | solution.py:22
  85.6 7.9 %all-to-all-done.3 = bf16[8,64,512]{2,1,0:T(8,128)(2,1)S(1)} async-done(((bf16[8,64,512]{2,1,0:T(8,128)(2,1)}), bf16[8,64,512]{2,1,0:T(8,128)(2,1)S(1)}, u32[]{:S(2)}, u32[]{:S(2)}) %all-to-all-start.3) | async-done | bytes 524320 | tf_op jit(solution)/shard_map/all_to_all | solution.py:22
  93.6 0.7 all_to_all.37
  94.3 3.9 %all-to-all-start.4 = ((bf16[32,2,512]{2,1,0:T(2,128)(2,1)}), bf16[32,2,512]{2,1,0:T(2,128)(2,1)S(1)}, u32[]{:S(2)}, u32[]{:S(2)}) async-start(bf16[32,2,512]{2,1,0:T(2,128)(2,1)} %all_to_all.37), calls=%async_computation.4 | async-start | bytes 131072 | tf_op jit(solution)/shard_map/all_to_all | solution.py:127
  98.2 0.6 pad_maximum_fusion.1
  98.8 9.9 %all-to-all-done.4 = bf16[32,2,512]{2,1,0:T(2,128)(2,1)S(1)} async-done(((bf16[32,2,512]{2,1,0:T(2,128)(2,1)}), bf16[32,2,512]{2,1,0:T(2,128)(2,1)S(1)}, u32[]{:S(2)}, u32[]{:S(2)}) %all-to-all-start.4) | async-done | bytes 65568 | tf_op jit(solution)/shard_map/all_to_all | solution.py:127
  108.7 0.7 gather_fusion.1
  109.5 0.8 fusion.20
  (42 shorter events, 1.2 us)
Async XLA Ops:
  0.6 55.1 %copy-start = (bf16[2,1,4096,128]{3,2,1,0:T(8,128)(2,1)S(1)}, bf16[2,1,4096,128]{3,2,1,0:T(8,128)(2,1)}, u32[]{:S(2)}) copy-start(bf16[2,1,4096,128]{3,2,1,0:T(8,128)(2,1)} %param.17) | copy-start | bytes 6291460
  0.6 27.3 %copy-start.2 = (bf16[512,128]{1,0:T(8,128)(2,1)S(1)}, bf16[512,128]{1,0:T(8,128)(2,1)}, u32[]{:S(2)}) copy-start(bf16[512,128]{1,0:T(8,128)(2,1)} %param.14) | copy-start | bytes 393220
  0.7 27.5 %copy-start.3 = (bf16[512,128]{1,0:T(8,128)(2,1)S(1)}, bf16[512,128]{1,0:T(8,128)(2,1)}, u32[]{:S(2)}) copy-start(bf16[512,128]{1,0:T(8,128)(2,1)} %param.15) | copy-start | bytes 393220
  28.0 5.5 %copy-start.4 = (s32[2]{0:T(128)S(1)}, s32[2]{0:T(128)}, u32[]{:S(2)}) copy-start(s32[2]{0:T(128)} %param.19) | copy-start | bytes 28
  29.5 25.0 %all-to-all-start.1 = ((f32[32,2,2304]{2,1,0:T(2,128)}), f32[32,2,2304]{2,1,0:T(2,128)S(1)}, u32[]{:S(2)}, u32[]{:S(2)}) async-start(f32[32,2,2304]{2,1,0:T(2,128)} %reshape.278), calls=%async_computation.1 | async-start | bytes 1179648 | tf_op jit(solution)/shard_map/all_to_all | solution.py:16
  54.7 2.0 %copy-start.5 = (bf16[2,1,4096,128]{3,2,1,0:T(8,128)(2,1)S(1)}, bf16[2,1,4096,128]{3,2,1,0:T(8,128)(2,1)}, u32[]{:S(2)}) copy-start(bf16[2,1,4096,128]{3,2,1,0:T(8,128)(2,1)} %param.18) | copy-start | bytes 6291460
  56.7 5.2 %copy-start.6 = (s32[32]{0:T(128)S(1)}, s32[32]{0:T(128)}, u32[]{:S(2)}) copy-start(s32[32]{0:T(128)} %param.12) | copy-start | bytes 388
  58.1 18.5 %all-to-all-start.2 = ((bf16[32,2,2048]{2,1,0:T(2,128)(2,1)}), bf16[32,2,2048]{2,1,0:T(2,128)(2,1)S(1)}, u32[]{:S(2)}, u32[]{:S(2)}) async-start(bf16[32,2,2048]{2,1,0:T(2,128)(2,1)} %broadcast_in_dim.81), calls=%async_computation.2 | async-start | bytes 524288 | tf_op jit(solution)/shard_map/all_to_all | solution.py:22
  78.8 30.7 %copy-start.1 = (bf16[2,16384]{1,0:T(2,128)(2,1)S(1)}, bf16[2,16384]{1,0:T(2,128)(2,1)}, u32[]{:S(2)}) copy-start(bf16[2,16384]{1,0:T(2,128)(2,1)} %param.10) | copy-start | bytes 196612
  79.6 13.9 %all-to-all-start.3 = ((bf16[8,64,512]{2,1,0:T(8,128)(2,1)}), bf16[8,64,512]{2,1,0:T(8,128)(2,1)S(1)}, u32[]{:S(2)}, u32[]{:S(2)}) async-start(bf16[8,64,512]{2,1,0:T(8,128)(2,1)} %broadcast_in_dim.82), calls=%async_computation.3 | async-start | bytes 1048576 | tf_op jit(solution)/shard_map/all_to_all | solution.py:22
  94.3 14.4 %all-to-all-start.4 = ((bf16[32,2,512]{2,1,0:T(2,128)(2,1)}), bf16[32,2,512]{2,1,0:T(2,128)(2,1)S(1)}, u32[]{:S(2)}, u32[]{:S(2)}) async-start(bf16[32,2,512]{2,1,0:T(2,128)(2,1)} %all_to_all.37), calls=%async_computation.4 | async-start | bytes 131072 | tf_op jit(solution)/shard_map/all_to_all | solution.py:127
where the time goes:
time: 112 us; the launch traced here: 110 us
  waiting for transfers between devices  51.7 us (46%)
  blocking collectives  20.8 us (19%)
  starting transfers between devices  17.5 us (16%)
  other arithmetic  8.38 us (7%)
  matrix products  5.76 us (5%)
  local copies, waits for them, and re-layouts  5.16 us (5%)
    all_to_all x2, waiting for transfers between devices, sent_to_all(): lax.all_to_all(jnp.broadcast_to(shard[None], (size, *shard.shape)), axis,...  20.9 us
    all_to_all x1, waiting for transfers between devices, summed_on_arrival(): lax.all_to_all(tiles, axis, split_axis=0, concat_axis=0, tiled=True)  20.8 us
    all_to_all x1, blocking collectives, body(): lax.all_to_all(arranged, 'group', split_axis=1, concat_axis=0, tiled=True)  20.8 us
    all_to_all x1, waiting for transfers between devices, body(): lax.all_to_all(summed.astype(jnp.bfloat16), 'group', split_axis=0, concat...  9.91 us
    all_to_all x2, starting transfers between devices, sent_to_all(): lax.all_to_all(jnp.broadcast_to(shard[None], (size, *shard.shape)), axis,...  9.8 us
    all_to_all x1, starting transfers between devices, summed_on_arrival(): lax.all_to_all(tiles, axis, split_axis=0, concat_axis=0, tiled=True)  3.89 us
    all_to_all x1, starting transfers between devices, body(): lax.all_to_all(summed.astype(jnp.bfloat16), 'group', split_axis=0, concat...  3.85 us
  transfers between devices with their start and end apart: 4, of which 4 were waited for; matrix products, arithmetic and copies ran while one was open for 2% of the time, Pallas kernels for 0%

commit v1 on v0

v1 whole, which is shorter than its diff:
```python
import math

import jax
import jax.numpy as jnp
from jax import lax
from jax.sharding import PartitionSpec as P

ROTARY_BASE = 500000.0


def rotate(values, angles):
    half_dim = values.shape[-1] // 2
    cosine = jnp.cos(angles)
    sine_part = jnp.sin(angles)
    first_half = values[..., :half_dim]
    second_half = values[..., half_dim:]
    return jnp.concatenate(
        [
            first_half * cosine - second_half * sine_part,
            second_half * cosine + first_half * sine_part,
        ],
        axis=-1,
    )


def angles_for(lengths, head_dim):
    half_dim = head_dim // 2
    frequency = jnp.exp(
        -math.log(ROTARY_BASE) * (2.0 * jnp.arange(half_dim, dtype=jnp.float32)) / head_dim
    )
    return lengths.astype(jnp.float32)[:, None] * frequency[None, :]


def exchange(tiles, axis, sets):
    return lax.all_to_all(tiles, axis, 0, 0, tiled=True, axis_index_groups=sets)


def attend(projected, k_cache, v_cache, lengths, query_cols, key_cols):
    sequences = projected.shape[0]
    head_dim = k_cache.shape[3]
    kv_local = k_cache.shape[1]
    queries = projected[:, :query_cols].reshape(sequences, query_cols // head_dim, head_dim)
    keys_new = projected[:, query_cols : query_cols + key_cols].reshape(
        sequences, kv_local, head_dim
    )
    values_new = projected[:, query_cols + key_cols :].reshape(sequences, kv_local, head_dim)
    angles = angles_for(lengths, head_dim)[:, None, :]
    new_keys = rotate(keys_new, angles).astype(jnp.bfloat16)
    new_values = values_new.astype(jnp.bfloat16)
    group_ratio = queries.shape[1] // kv_local
    scaled = (
        (rotate(queries, angles) / math.sqrt(head_dim))
        .astype(jnp.bfloat16)
        .reshape(sequences, kv_local, group_ratio, head_dim)
    )
    scores = jnp.einsum("bgrd,bgld->bgrl", scaled, k_cache, preferred_element_type=jnp.float32)
    own_score = jnp.einsum("bgrd,bgd->bgr", scaled, new_keys, preferred_element_type=jnp.float32)
    visible = (jnp.arange(k_cache.shape[2])[None, :] < lengths[:, None])[:, None, None, :]
    masked = jnp.where(visible, scores, -1e30)
    highest = jnp.maximum(jnp.max(masked, axis=-1), own_score)
    exponent = jnp.where(visible, jnp.exp(masked - highest[..., None]), 0.0)
    own_exp = jnp.exp(own_score - highest)
    denominator = jnp.sum(exponent, axis=-1) + own_exp
    weights = (exponent / denominator[..., None]).astype(jnp.bfloat16)
    own_weight = (own_exp / denominator).astype(jnp.bfloat16)
    combined = jnp.einsum("bgrl,bgld->bgrd", weights, v_cache, preferred_element_type=jnp.float32)
    combined = (
        combined
        + own_weight.astype(jnp.float32)[..., None] * new_values.astype(jnp.float32)[:, :, None, :]
    )
    attended = combined.astype(jnp.bfloat16).reshape(sequences, query_cols)
    return attended, new_keys, new_values


def solution(mesh):
    groups = mesh.shape["group"]
    tensors = mesh.shape["tensor"]
    chips = groups // 2
    half = chips // 2
    partner = [(i, i ^ 1) for i in range(groups)]
    same_core = [[2 * chip + core for chip in range(chips)] for core in range(2)]
    near = [
        [
            (2 * chip + core) * tensors + (pair * 2 + ((chip // half) ^ side))
            for chip in range(chips)
        ]
        for core in range(2)
        for pair in range(tensors // 2)
        for side in range(2)
    ]

    def body(
        hidden, norm_gain, slab_of, w_query, w_key, w_value, w_out, k_cache, v_cache, lengths
    ):
        sequences, model_width = hidden.shape
        slab_width = model_width // groups
        core = lax.axis_index("group") % 2
        other_query, other_key, other_value, other_out = (
            lax.ppermute(w, "group", partner) for w in (w_query, w_key, w_value, w_out)
        )
        order = slab_of.reshape(chips, 2)
        order = jnp.where(core == 0, order, order[:, ::-1]).reshape(-1)
        hidden_wide = hidden.astype(jnp.float32)
        mean_square = jnp.mean(hidden_wide * hidden_wide, axis=1, keepdims=True)
        normed = (hidden_wide * lax.rsqrt(mean_square + 1e-05) * norm_gain).astype(jnp.bfloat16)
        arranged = jnp.take(normed.reshape(sequences, groups, slab_width), order, axis=1)
        arranged = jnp.swapaxes(arranged.reshape(sequences, chips, 2 * slab_width), 0, 1)
        columns = exchange(arranged, ("group", "tensor"), near).reshape(
            chips * sequences, 2 * slab_width
        )
        own, other = columns[:, :slab_width], columns[:, slab_width:]

        def project(w, w_other):
            return jnp.dot(own, w, preferred_element_type=jnp.float32) + jnp.dot(
                other, w_other, preferred_element_type=jnp.float32
            )

        partial = jnp.concatenate(
            [
                project(w_query, other_query),
                project(w_key, other_key),
                project(w_value, other_value),
            ],
            axis=1,
        ).reshape(chips, sequences, -1)
        projected = exchange(partial, "group", same_core).sum(axis=0)
        attended, new_keys, new_values = attend(
            projected, k_cache, v_cache, lengths, w_query.shape[1], w_key.shape[1]
        )
        gathered = exchange(
            jnp.broadcast_to(attended[None], (chips, *attended.shape)), "group", same_core
        ).reshape(chips * sequences, -1)
        head_partial = jnp.concatenate(
            [
                jnp.dot(gathered, w_out, preferred_element_type=jnp.float32),
                jnp.dot(gathered, other_out, preferred_element_type=jnp.float32),
            ],
            axis=1,
        ).astype(jnp.bfloat16)
        returned = exchange(
            head_partial.reshape(chips, sequences, 2 * slab_width), "group", same_core
        )
        everyone = lax.all_to_all(
            jnp.broadcast_to(returned[None], (tensors, *returned.shape)), "tensor", 0, 0, tiled=True
        )
        summed = jnp.sum(everyone.astype(jnp.float32), axis=0)
        summed = jnp.swapaxes(summed, 0, 1).reshape(sequences, groups, slab_width)
        ordered = jnp.take(summed, jnp.argsort(order), axis=1).reshape(sequences, model_width)
        out_hidden = (hidden_wide + ordered).astype(jnp.bfloat16)
        return (out_hidden, new_keys, new_values)

    in_specs = (
        P("group", None),
        P(),
        P(),
        P("group", "tensor"),
        P("group", "tensor"),
        P("group", "tensor"),
        P("tensor", "group"),
        P("group", "tensor", None, None),
        P("group", "tensor", None, None),
        P("group"),
    )
    out_specs = (P("group", None), P("group", "tensor", None), P("group", "tensor", None))
    return jax.shard_map(body, mesh=mesh, in_specs=in_specs, out_specs=out_specs, check_vma=False)
```

time: 112 us -> 99.9 us (0.89)
  blocking collectives: 20.8 us -> 0 us
  starting transfers between devices: 17.5 us -> 29.5 us
  waiting for transfers between devices: 51.7 us -> 44.3 us
  matrix products: 5.76 us -> 11 us
    all_to_all x1 -> x0, blocking collectives: 20.8 us -> none  [body(): lax.all_to_all(arranged, 'group', split_axis=1, concat_axis=0, tiled=True)]
    all_to_all x4 -> x5, starting transfers between devices: 17.5 us -> 28.7 us  [the longest x4 22.2 us: exchange(): return lax.all_to_all(tiles, axis, 0, 0, tiled=True, axis_index_groups=sets)]
    all_to_all x4 -> x5, waiting for transfers between devices: 51.7 us -> 44.2 us  [the longest x4 37.4 us: exchange(): return lax.all_to_all(tiles, axis, 0, 0, tiled=True, axis_index_groups=sets)]
    dot_general x7 -> x11, matrix products: 5.76 us -> 11 us  [the longest x3 3.24 us: project(): jnp.dot(own, w, preferred_element_type=jnp.float32)]
  transfers between devices with their start and end apart: 4 -> 9, of which waited for: 4 -> 5; matrix products, arithmetic and copies ran while one was open for 2% -> 19% of each run, Pallas kernels for 0% -> 0%
where the time goes in v1:
time: 99.9 us; the launch traced here: 99.2 us
  waiting for transfers between devices  44.3 us (44%)
  starting transfers between devices  29.5 us (30%)
  matrix products  11 us (11%)
  other arithmetic  7.43 us (7%)
  local copies, waits for them, and re-layouts  6.07 us (6%)
    all_to_all x4, waiting for transfers between devices, exchange(): return lax.all_to_all(tiles, axis, 0, 0, tiled=True, axis_index_groups=sets)  37.4 us
    all_to_all x4, starting transfers between devices, exchange(): return lax.all_to_all(tiles, axis, 0, 0, tiled=True, axis_index_groups=sets)  22.2 us
    all_to_all x1, waiting for transfers between devices, body(): lax.all_to_all(jnp.broadcast_to(returned[None], (tensors, *returned.shape...  6.81 us
    all_to_all x1, starting transfers between devices, body(): lax.all_to_all(jnp.broadcast_to(returned[None], (tensors, *returned.shape...  6.48 us
    dot_general x3, matrix products, project(): jnp.dot(own, w, preferred_element_type=jnp.float32)  3.24 us
    dot_general x3, matrix products, project(): jnp.dot(other, w_other, preferred_element_type=jnp.float32)  2.33 us
    dot_general x1, matrix products, body(): jnp.dot(gathered, other_out, preferred_element_type=jnp.float32)  2.05 us
    dot_general x1, matrix products, body(): jnp.dot(gathered, w_out, preferred_element_type=jnp.float32)  2.04 us
  transfers between devices with their start and end apart: 9, of which 5 were waited for; matrix products, arithmetic and copies ran while one was open for 19% of the time, Pallas kernels for 0%

profile of v1, /device:TPU:2, one launch (start us, length us, event | category | flops | bytes accessed | tf_op | source)
XLA Modules:
  0.0 99.2 jit_solution(15325780856714951034)
XLA Ops:
  0.8 0.9 reshape.315
  1.7 1.1 %fusion.27 = f32[2]{0:T(128)S(1)} fusion(bf16[2,16384]{1,0:T(2,128)(2,1)} %param.10), kind=kLoop, calls=%fused_computation.30 | loop fusion | flops 98302 | bytes 65544 | tf_op jit(solution)/shard_map/reduce_sum | solution.py:104
  2.8 1.0 %fusion.29 = bf16[2,16384]{1,0:T(2,128)(2,1)S(1)} fusion(bf16[2,16384]{1,0:T(2,128)(2,1)} %param.10, f32[2]{0:T(128)S(1)} %add_rsqrt_fusion, f32[16384]{0:T(1024)} %param.11), kind=kLoop, calls=%fused_computation.32 | loop fusion | flops 131072 | bytes 196616 | tf_op jit(solution)/shard_map/convert_element_type | solution.py:105
  4.1 0.7 gather_fusion
  4.8 0.7 fusion.33
  5.5 9.5 %all-to-all-start = ((bf16[16,2,1024]{2,1,0:T(2,128)(2,1)}), bf16[16,2,1024]{2,1,0:T(2,128)(2,1)S(1)}, u32[]{:S(2)}, u32[]{:S(2)}) async-start(bf16[16,2,1024]{2,1,0:T(2,128)(2,1)} %fusion.33), calls=%async_computation | async-start | bytes 131072 | tf_op jit(solution)/shard_map/all_to_all | solution.py:35
  15.2 0.4 collective-permute-start.1
  15.7 7.8 %all-to-all-done = bf16[16,2,1024]{2,1,0:T(2,128)(2,1)S(1)} async-done(((bf16[16,2,1024]{2,1,0:T(2,128)(2,1)}), bf16[16,2,1024]{2,1,0:T(2,128)(2,1)S(1)}, u32[]{:S(2)}, u32[]{:S(2)}) %all-to-all-start) | async-done | bytes 65568 | tf_op jit(solution)/shard_map/all_to_all | solution.py:35
  23.6 1.0 %fusion.37 = f32[32,128]{1,0:T(8,128)S(1)} fusion(bf16[512,128]{1,0:T(8,128)(2,1)} %param.15, bf16[32,1024]{1,0:T(8,128)(2,1)S(1)} %reshape.319), kind=kOutput, calls=%fused_computation.44 | convolution fusion | flops 4194304 | bytes 180224 | tf_op jit(solution)/shard_map/dot_general | solution.py:114
  24.6 2.1 %fusion.41 = f32[32,2048]{1,0:T(8,128)S(1)} fusion(bf16[512,2048]{1,0:T(8,128)(2,1)} %param.13, bf16[32,1024]{1,0:T(8,128)(2,1)S(1)} %reshape.319), kind=kOutput, calls=%fused_computation.48 | convolution fusion | flops 67108864 | bytes 2392064 | tf_op jit(solution)/shard_map/dot_general | solution.py:114
  27.2 2.1 %convolution_add_fusion = f32[32,2048]{1,0:T(8,128)S(1)} fusion(f32[32,2048]{1,0:T(8,128)S(1)} %fusion.41, bf16[512,2048]{1,0:T(8,128)(2,1)} %collective-permute-done, bf16[32,1024]{1,0:T(8,128)(2,1)S(1)} %reshape.319), kind=kOutput, calls=%fused_computation.3 | convolution fusion | flops 67174400 | bytes 2654208 | tf_op jit(solution)/shard_map/dot_general | solution.py:114
  29.2 0.9 reshape.320
  30.1 4.4 %all-to-all-start.1 = ((f32[16,2,2304]{2,1,0:T(2,128)}), f32[16,2,2304]{2,1,0:T(2,128)S(1)}, u32[]{:S(2)}, u32[]{:S(2)}) async-start(f32[16,2,2304]{2,1,0:T(2,128)} %reshape.320), calls=%async_computation.1 | async-start | bytes 589824 | tf_op jit(solution)/shard_map/all_to_all | solution.py:35
  34.8 11.2 %all-to-all-done.1 = f32[16,2,2304]{2,1,0:T(2,128)S(1)} async-done(((f32[16,2,2304]{2,1,0:T(2,128)}), f32[16,2,2304]{2,1,0:T(2,128)S(1)}, u32[]{:S(2)}, u32[]{:S(2)}) %all-to-all-start.1) | async-done | bytes 294944 | tf_op jit(solution)/shard_map/all_to_all | solution.py:35
  46.7 0.7 fusion.60
  47.7 0.5 fusion.58
  48.2 0.5 fusion.19
  48.7 0.7 broadcast_in_dim.84
  49.4 4.7 %all-to-all-start.2 = ((bf16[16,2,2048]{2,1,0:T(2,128)(2,1)}), bf16[16,2,2048]{2,1,0:T(2,128)(2,1)S(1)}, u32[]{:S(2)}, u32[]{:S(2)}) async-start(bf16[16,2,2048]{2,1,0:T(2,128)(2,1)} %broadcast_in_dim.84), calls=%async_computation.2 | async-start | bytes 262144 | tf_op jit(solution)/shard_map/all_to_all | solution.py:35
  54.3 1.6 %sort.17 = (s32[32]{0:T(128)}, s32[32]{0:T(128)S(1)}) sort(s32[32]{0:T(128)S(1)} %reshape.316, s32[32]{0:T(128)S(1)} %iota.18), dimensions={0}, to_apply=%region_0.1 | sort | flops 160 | bytes 512 | tf_op jit(solution)/shard_map/jit(argsort)/sort | solution.py:148
  55.9 8.4 %all-to-all-done.2 = bf16[16,2,2048]{2,1,0:T(2,128)(2,1)S(1)} async-done(((bf16[16,2,2048]{2,1,0:T(2,128)(2,1)}), bf16[16,2,2048]{2,1,0:T(2,128)(2,1)S(1)}, u32[]{:S(2)}, u32[]{:S(2)}) %all-to-all-start.2) | async-done | bytes 131104 | tf_op jit(solution)/shard_map/all_to_all | solution.py:35
  64.2 2.0 %fusion.7 = bf16[16,2,512]{2,0,1:T(8,128)(2,1)S(1)} fusion(bf16[2048,512]{1,0:T(8,128)(2,1)} %param.16, bf16[16,2,2048]{2,1,0:T(2,128)(2,1)S(1)} %all-to-all-done.2), kind=kOutput, calls=%fused_computation.11 | convolution fusion | flops 67125248 | bytes 2260992 | tf_op jit(solution)/shard_map/dot_general | solution.py:135
  66.3 2.0 %fusion.10 = bf16[16,2,512]{2,0,1:T(8,128)(2,1)S(1)} fusion(bf16[2048,512]{1,0:T(8,128)(2,1)} %collective-permute-done.3, bf16[16,2,2048]{2,1,0:T(2,128)(2,1)S(1)} %all-to-all-done.2), kind=kOutput, calls=%fused_computation.12 | convolution fusion | flops 67125248 | bytes 2260992 | tf_op jit(solution)/shard_map/dot_general | solution.py:136
  68.4 0.7 copy.22
  69.1 3.5 %all-to-all-start.3 = ((bf16[16,2,1024]{2,1,0:T(2,128)(2,1)}), bf16[16,2,1024]{2,1,0:T(2,128)(2,1)S(1)}, u32[]{:S(2)}, u32[]{:S(2)}) async-start(bf16[16,2,1024]{2,1,0:T(2,128)(2,1)} %copy.22), calls=%async_computation.3 | async-start | bytes 131072 | tf_op jit(solution)/shard_map/all_to_all | solution.py:35
  72.6 10.0 %all-to-all-done.3 = bf16[16,2,1024]{2,1,0:T(2,128)(2,1)S(1)} async-done(((bf16[16,2,1024]{2,1,0:T(2,128)(2,1)}), bf16[16,2,1024]{2,1,0:T(2,128)(2,1)S(1)}, u32[]{:S(2)}, u32[]{:S(2)}) %all-to-all-start.3) | async-done | bytes 65568 | tf_op jit(solution)/shard_map/all_to_all | solution.py:35
  82.6 0.8 broadcast_in_dim.85
  83.5 6.5 %all-to-all-start.4 = ((bf16[8,16,2,1024]{3,1,2,0:T(8,128)(2,1)}), bf16[8,16,2,1024]{3,1,2,0:T(8,128)(2,1)S(1)}, u32[]{:S(2)}, u32[]{:S(2)}) async-start(bf16[8,16,2,1024]{3,1,2,0:T(8,128)(2,1)} %broadcast_in_dim.85), calls=%async_computation.4 | async-start | bytes 1048576 | tf_op jit(solution)/shard_map/all_to_all | solution.py:143
  90.1 0.6 pad_maximum_fusion.2
  90.7 6.8 %all-to-all-done.4 = bf16[8,16,2,1024]{3,1,2,0:T(8,128)(2,1)S(1)} async-done(((bf16[8,16,2,1024]{3,1,2,0:T(8,128)(2,1)}), bf16[8,16,2,1024]{3,1,2,0:T(8,128)(2,1)S(1)}, u32[]{:S(2)}, u32[]{:S(2)}) %all-to-all-start.4) | async-done | bytes 524320 | tf_op jit(solution)/shard_map/all_to_all | solution.py:143
  97.7 0.7 gather_fusion.1
  98.4 0.8 fusion.30
  (59 shorter events, 2.7 us)
Async XLA Ops:
  0.6 46.0 %copy-start = (bf16[2,1,4096,128]{3,2,1,0:T(8,128)(2,1)S(1)}, bf16[2,1,4096,128]{3,2,1,0:T(8,128)(2,1)}, u32[]{:S(2)}) copy-start(bf16[2,1,4096,128]{3,2,1,0:T(8,128)(2,1)} %param.17) | copy-start | bytes 6291460
  0.6 26.0 %copy-start.2 = (bf16[512,128]{1,0:T(8,128)(2,1)S(1)}, bf16[512,128]{1,0:T(8,128)(2,1)}, u32[]{:S(2)}) copy-start(bf16[512,128]{1,0:T(8,128)(2,1)} %param.14) | copy-start | bytes 393220
  0.7 26.5 %collective-permute-start = (bf16[512,2048]{1,0:T(8,128)(2,1)}, bf16[512,2048]{1,0:T(8,128)(2,1)}, u32[]{:S(2)}, u32[]{:S(2)}) collective-permute-start(bf16[512,2048]{1,0:T(8,128)(2,1)} %param.13), channel_id=1, source_target_pairs={{0,8},{8,0},{16,24},{24,16},{32,40},{40,32},{48,56},{56,48},{64,72... | collective-permute-start | bytes 6291464 | tf_op jit(solution)/shard_map/ppermute | solution.py:99
  5.5 18.0 %all-to-all-start = ((bf16[16,2,1024]{2,1,0:T(2,128)(2,1)}), bf16[16,2,1024]{2,1,0:T(2,128)(2,1)S(1)}, u32[]{:S(2)}, u32[]{:S(2)}) async-start(bf16[16,2,1024]{2,1,0:T(2,128)(2,1)} %fusion.33), calls=%async_computation | async-start | bytes 131072 | tf_op jit(solution)/shard_map/all_to_all | solution.py:35
  15.0 11.8 %collective-permute-start.2 = (bf16[512,128]{1,0:T(8,128)(2,1)}, bf16[512,128]{1,0:T(8,128)(2,1)S(1)}, u32[]{:S(2)}, u32[]{:S(2)}) collective-permute-start(bf16[512,128]{1,0:T(8,128)(2,1)} %param.15), channel_id=1, source_target_pairs={{0,8},{8,0},{16,24},{24,16},{32,40},{40,32},{48,56},{56,48},{64,72... | collective-permute-start | bytes 393224 | tf_op jit(solution)/shard_map/ppermute | solution.py:99
  15.2 11.8 %collective-permute-start.1 = (bf16[512,128]{1,0:T(8,128)(2,1)}, bf16[512,128]{1,0:T(8,128)(2,1)S(1)}, u32[]{:S(2)}, u32[]{:S(2)}) collective-permute-start(bf16[512,128]{1,0:T(8,128)(2,1)} %param.14), channel_id=1, source_target_pairs={{0,8},{8,0},{16,24},{24,16},{32,40},{40,32},{48,56},{56,48},{64,72... | collective-permute-start | bytes 393224 | tf_op jit(solution)/shard_map/ppermute | solution.py:99
  15.6 50.7 %collective-permute-start.3 = (bf16[2048,512]{1,0:T(8,128)(2,1)}, bf16[2048,512]{1,0:T(8,128)(2,1)}, u32[]{:S(2)}, u32[]{:S(2)}) collective-permute-start(bf16[2048,512]{1,0:T(8,128)(2,1)} %param.16), channel_id=1, source_target_pairs={{0,8},{8,0},{16,24},{24,16},{32,40},{40,32},{48,56},{56,48},{64,72... | collective-permute-start | bytes 6291464 | tf_op jit(solution)/shard_map/ppermute | solution.py:99
  27.1 7.5 %copy-start.3 = (s32[2]{0:T(128)S(1)}, s32[2]{0:T(128)}, u32[]{:S(2)}) copy-start(s32[2]{0:T(128)} %param.19) | copy-start | bytes 28
  30.1 15.9 %all-to-all-start.1 = ((f32[16,2,2304]{2,1,0:T(2,128)}), f32[16,2,2304]{2,1,0:T(2,128)S(1)}, u32[]{:S(2)}, u32[]{:S(2)}) async-start(f32[16,2,2304]{2,1,0:T(2,128)} %reshape.320), calls=%async_computation.1 | async-start | bytes 589824 | tf_op jit(solution)/shard_map/all_to_all | solution.py:35
  46.2 2.1 %copy-start.4 = (bf16[2,1,4096,128]{3,2,1,0:T(8,128)(2,1)S(1)}, bf16[2,1,4096,128]{3,2,1,0:T(8,128)(2,1)}, u32[]{:S(2)}) copy-start(bf16[2,1,4096,128]{3,2,1,0:T(8,128)(2,1)} %param.18) | copy-start | bytes 6291460
  49.4 14.8 %all-to-all-start.2 = ((bf16[16,2,2048]{2,1,0:T(2,128)(2,1)}), bf16[16,2,2048]{2,1,0:T(2,128)(2,1)S(1)}, u32[]{:S(2)}, u32[]{:S(2)}) async-start(bf16[16,2,2048]{2,1,0:T(2,128)(2,1)} %broadcast_in_dim.84), calls=%async_computation.2 | async-start | bytes 262144 | tf_op jit(solution)/shard_map/all_to_all | solution.py:35
  68.3 30.1 %copy-start.1 = (bf16[2,16384]{1,0:T(2,128)(2,1)S(1)}, bf16[2,16384]{1,0:T(2,128)(2,1)}, u32[]{:S(2)}) copy-start(bf16[2,16384]{1,0:T(2,128)(2,1)} %param.10) | copy-start | bytes 196612
  69.1 13.5 %all-to-all-start.3 = ((bf16[16,2,1024]{2,1,0:T(2,128)(2,1)}), bf16[16,2,1024]{2,1,0:T(2,128)(2,1)S(1)}, u32[]{:S(2)}, u32[]{:S(2)}) async-start(bf16[16,2,1024]{2,1,0:T(2,128)(2,1)} %copy.22), calls=%async_computation.3 | async-start | bytes 131072 | tf_op jit(solution)/shard_map/all_to_all | solution.py:35
  83.5 14.0 %all-to-all-start.4 = ((bf16[8,16,2,1024]{3,1,2,0:T(8,128)(2,1)}), bf16[8,16,2,1024]{3,1,2,0:T(8,128)(2,1)S(1)}, u32[]{:S(2)}, u32[]{:S(2)}) async-start(bf16[8,16,2,1024]{3,1,2,0:T(8,128)(2,1)} %broadcast_in_dim.85), calls=%async_computation.4 | async-start | bytes 1048576 | tf_op jit(solution)/shard_map/all_to_all | solution.py:143

commit v2 on v1

v2 whole, which is shorter than its diff:
```python
import functools
import math

import jax
import jax.numpy as jnp
from jax import lax
from jax.experimental import pallas as pl
from jax.experimental.pallas import tpu as pltpu
from jax.sharding import PartitionSpec as P

ROTARY_BASE = 500000.0
EPSILON = 1e-05
LANES = 128
WIDE = jnp.float32
NARROW = jnp.bfloat16


def in_vmem(*arrays):
    return [pltpu.with_memory_space_constraint(a, pltpu.VMEM) for a in arrays]


def in_hbm(*arrays):
    return [pltpu.with_memory_space_constraint(a, pltpu.HBM) for a in arrays]


def call(kernel, outs, scalars, arrays, scratch=(), far=(), **sizes):
    def at(space, operands):
        return [pl.BlockSpec(memory_space=space)] * len(operands)

    return pl.pallas_call(
        functools.partial(kernel, **sizes),
        out_shape=outs,
        in_specs=at(pltpu.SMEM, scalars) + at(pltpu.HBM, far) + at(pltpu.VMEM, arrays),
        out_specs=jax.tree.map(lambda _: pl.BlockSpec(memory_space=pltpu.VMEM), outs),
        scratch_shapes=list(scratch),
        compiler_params=pltpu.CompilerParams(vmem_limit_bytes=8 * 1024 * 1024),
        name=kernel.__name__,
    )(*scalars, *in_hbm(*far), *arrays)


def arrange(core_ref, *refs, slab):
    far, refs = refs[:7], refs[7:]
    out_ref, cos_ref, sin_ref, *kept, slab_ref, length_ref, hidden_ref, gain_ref, rows_ref, sems = refs
    near = (hidden_ref, gain_ref, slab_ref, length_ref, *kept)
    copies = [pltpu.make_async_copy(f, n, sems.at[i]) for i, (f, n) in enumerate(zip(far, near))]
    for copy in copies:
        copy.start()
    copies, later = copies[:4], copies[4:]
    sequences, width = hidden_ref.shape
    head_dim = cos_ref.shape[1]
    core = core_ref[0]
    lane = lax.broadcasted_iota(jnp.int32, (1, head_dim), 1)
    half_dim = head_dim // 2
    place_in_half = jnp.where(lane < half_dim, lane, lane - half_dim).astype(WIDE)
    frequency = jnp.exp(-math.log(ROTARY_BASE) * (2.0 * place_in_half) / head_dim)
    for copy in copies:
        copy.wait()
    squares = jnp.zeros((sequences, slab), WIDE)
    for first in range(0, width, slab):
        x = hidden_ref[:, first : first + slab].astype(WIDE)
        squares = squares + x * x
    scale = lax.rsqrt(jnp.sum(squares, axis=1, keepdims=True) / width + EPSILON)
    chips, lines = out_ref.shape[:2]
    pieces = slab // LANES
    for chip in range(chips):
        for place in range(2):
            index = 2 * chip + (core if place == 0 else 1 - core)
            first = pl.multiple_of(slab_ref[index] * slab, slab)
            x = hidden_ref[:, pl.ds(first, slab)].astype(WIDE)
            x = x * scale * gain_ref[:, pl.ds(first, slab)]
            for piece in range(pieces):
                line = chip * lines + place * pieces + piece
                rows_ref[pl.ds(line, sequences, stride=lines // sequences), :] = x[
                    :, piece * LANES : (piece + 1) * LANES
                ]
    for chip in range(chips):
        out_ref[chip] = rows_ref[chip * lines : (chip + 1) * lines, :].astype(NARROW)
    for s in range(sequences):
        angle = length_ref[s].astype(WIDE) * frequency
        cos_ref[s : s + 1, :] = jnp.cos(angle)
        sine = jnp.sin(angle)
        sin_ref[s : s + 1, :] = jnp.where(lane < half_dim, -sine, sine)
    for copy in later:
        copy.wait()


def rows_of(x_ref, wide_ref, pieces):
    sources, lines = x_ref.shape[:2]
    for source in range(sources):
        wide_ref[source * lines : (source + 1) * lines, :] = x_ref[source].astype(WIDE)
    rows = sources * lines // pieces
    return jnp.concatenate(
        [wide_ref[pl.ds(p, rows, stride=pieces), :].astype(NARROW) for p in range(pieces)], axis=1
    )


def project(x_ref, *refs, chunk):
    *weights, out_ref, wide_ref = refs
    depth = weights[0].shape[0]
    x = rows_of(x_ref, wide_ref, 2 * depth // LANES)
    own, other = x[:, :depth], x[:, depth:]
    rows = out_ref.shape[1]
    offset = 0
    for mine, partners in zip(weights[0::2], weights[1::2]):
        step = min(chunk, mine.shape[1])
        for first in range(0, mine.shape[1], step):
            part = jnp.dot(own, mine[:, first : first + step], preferred_element_type=WIDE)
            part += jnp.dot(other, partners[:, first : first + step], preferred_element_type=WIDE)
            for chip in range(out_ref.shape[0]):
                out_ref[chip, :, offset : offset + step] = part[chip * rows : (chip + 1) * rows]
            offset += step


def attend(
    length_ref, part_ref, cos_ref, sin_ref, k_ref, v_ref, out_ref, key_ref, value_ref, heads_ref,
    *, heads
):
    sequences = part_ref.shape[1]
    head_dim = k_ref.shape[3]
    cached = k_ref.shape[2]
    total = part_ref[0]
    for source in range(1, part_ref.shape[0]):
        total = total + part_ref[source]
    for s in range(sequences):
        for h in range(heads + 2):
            heads_ref[s, h : h + 1, :] = total[s : s + 1, h * head_dim : (h + 1) * head_dim]
    value_ref[...] = total[:, (heads + 1) * head_dim :].astype(NARROW)
    new_keys = []
    for s in range(sequences):
        cosine, sine = cos_ref[s : s + 1], sin_ref[s : s + 1]

        def rotate(x):
            return x * cosine + pltpu.roll(x, head_dim // 2, 1) * sine

        query = rotate(heads_ref[s, :heads, :])
        scaled = (query / math.sqrt(head_dim)).astype(NARROW)
        new_key = rotate(heads_ref[s, heads : heads + 1, :]).astype(NARROW)
        new_value = heads_ref[s, heads + 1 : heads + 2, :].astype(NARROW)
        new_keys.append(new_key.astype(WIDE))
        scores = lax.dot_general(
            scaled, k_ref[s, 0], (((1,), (1,)), ((), ())), preferred_element_type=WIDE
        )
        own_score = jnp.sum(scaled.astype(WIDE) * new_key.astype(WIDE), axis=1, keepdims=True)
        visible = lax.broadcasted_iota(jnp.int32, (heads, cached), 1) < length_ref[s]
        masked = jnp.where(visible, scores, -1e30)
        highest = jnp.maximum(jnp.max(masked, axis=1, keepdims=True), own_score)
        exponent = jnp.where(visible, jnp.exp(masked - highest), 0.0)
        own_exp = jnp.exp(own_score - highest)
        share = 1.0 / (jnp.sum(exponent, axis=1, keepdims=True) + own_exp)
        weights = (exponent * share).astype(NARROW)
        own_weight = (own_exp * share).astype(NARROW)
        combined = jnp.dot(weights, v_ref[s, 0], preferred_element_type=WIDE)
        combined = combined + own_weight.astype(WIDE) * new_value.astype(WIDE)
        attended = combined.astype(NARROW)
        for target in range(out_ref.shape[0]):
            out_ref[target, s * heads : (s + 1) * heads, :] = attended
    key_ref[...] = jnp.concatenate(new_keys, axis=0).astype(NARROW)


def project_out(x_ref, w_ref, other_ref, out_ref, rows_ref, parts_ref, *, heads):
    chips, lines = out_ref.shape[:2]
    x = rows_of(x_ref, rows_ref, heads)
    rows = x.shape[0]
    slab = w_ref.shape[1]
    pieces = slab // LANES
    for place, w in enumerate((w_ref, other_ref)):
        part = jnp.dot(x, w[...], preferred_element_type=WIDE)
        for piece in range(pieces):
            parts_ref[pl.ds(place * pieces + piece, rows, stride=2 * pieces), :] = part[
                :, piece * LANES : (piece + 1) * LANES
            ]
    for chip in range(chips):
        out_ref[chip] = parts_ref[chip * lines : (chip + 1) * lines, :].astype(NARROW)


def repeat(x_ref, out_ref):
    for chip in range(x_ref.shape[0]):
        x = x_ref[chip]
        for target in range(out_ref.shape[0]):
            out_ref[target, chip] = x


def finish(core_ref, slab_ref, parts_ref, hidden_ref, out_ref, sums_ref, *, slab):
    core = core_ref[0]
    chips, lines = parts_ref.shape[1:3]
    sequences = hidden_ref.shape[0]
    pieces = slab // LANES
    for chip in range(chips):
        total = parts_ref[0, chip].astype(WIDE)
        for source in range(1, parts_ref.shape[0]):
            total = total + parts_ref[source, chip].astype(WIDE)
        sums_ref[chip * lines : (chip + 1) * lines, :] = total
    for chip in range(chips):
        for place in range(2):
            index = 2 * chip + (core if place == 0 else 1 - core)
            first = slab_ref[index] * slab
            for piece in range(pieces):
                line = chip * lines + place * pieces + piece
                added = sums_ref[pl.ds(line, sequences, stride=lines // sequences), :]
                at = pl.ds(pl.multiple_of(first + piece * LANES, LANES), LANES)
                out_ref[:, at] = (hidden_ref[:, at].astype(WIDE) + added).astype(NARROW)


def exchange(tiles, axis, sets):
    return lax.all_to_all(tiles, axis, 0, 0, tiled=True, axis_index_groups=sets)


def solution(mesh):
    groups = mesh.shape["group"]
    tensors = mesh.shape["tensor"]
    chips = groups // 2
    half = chips // 2
    partner = [(i, i ^ 1) for i in range(groups)]
    same_core = [[2 * chip + core for chip in range(chips)] for core in range(2)]
    near = [
        [
            (2 * chip + core) * tensors + (pair * 2 + ((chip // half) ^ side))
            for chip in range(chips)
        ]
        for core in range(2)
        for pair in range(tensors // 2)
        for side in range(2)
    ]

    def body(
        hidden, norm_gain, slab_of, w_query, w_key, w_value, w_out, k_cache, v_cache, lengths
    ):
        sequences, width = hidden.shape
        slab = width // groups
        head_dim = k_cache.shape[3]
        heads = w_query.shape[1] // head_dim
        columns = w_query.shape[1] + w_key.shape[1] + w_value.shape[1]
        core = (lax.axis_index("group") % 2).reshape(1)
        other_query, other_key, other_value, other_out = (
            lax.ppermute(w, "group", partner) for w in (w_query, w_key, w_value, w_out)
        )
        lines = sequences * 2 * slab // LANES
        arranged, cosine, sine, near_query, near_key, near_value = call(
            arrange,
            (
                pltpu.VMEM((chips, lines, LANES), NARROW),
                pltpu.VMEM((sequences, head_dim), WIDE),
                pltpu.VMEM((sequences, head_dim), WIDE),
                *(pltpu.VMEM(w.shape, NARROW) for w in (w_query, w_key, w_value)),
            ),
            (core,),
            (),
            [
                pltpu.SMEM((groups,), jnp.int32),
                pltpu.SMEM((sequences,), jnp.int32),
                pltpu.VMEM((sequences, width), NARROW),
                pltpu.VMEM((1, width), WIDE),
                pltpu.VMEM((chips * lines, LANES), WIDE),
                pltpu.SemaphoreType.DMA((7,)),
            ],
            (hidden, norm_gain.reshape(1, width), slab_of, lengths, w_query, w_key, w_value),
            slab=slab,
        )
        features = exchange(arranged, ("group", "tensor"), near)
        features, other_query, other_key, other_value, other_out = lax.optimization_barrier(
            (features, other_query, other_key, other_value, other_out)
        )
        partial = call(
            project,
            pltpu.VMEM((chips, sequences, columns), WIDE),
            (),
            (
                features,
                near_query, *in_vmem(other_query), near_key, *in_vmem(other_key), near_value, *in_vmem(other_value),
            ),
            [pltpu.VMEM((chips * lines, LANES), WIDE)],
            chunk=512,
        )
        parts = exchange(partial, "group", same_core)
        attended, new_keys, new_values = call(
            attend,
            (
                pltpu.VMEM((chips, sequences * heads, head_dim), NARROW),
                jax.ShapeDtypeStruct((sequences, head_dim), NARROW),
                jax.ShapeDtypeStruct((sequences, head_dim), NARROW),
            ),
            (lengths,),
            (parts, cosine, sine, *in_vmem(k_cache, v_cache)),
            [pltpu.VMEM((sequences, heads + 8, head_dim), WIDE)],
            heads=heads,
        )
        gathered = exchange(attended, "group", same_core)
        head_partial = call(
            project_out,
            pltpu.VMEM((chips, lines, LANES), NARROW),
            (),
            (gathered, *in_vmem(w_out, other_out)),
            [
                pltpu.VMEM((chips * sequences * heads, head_dim), WIDE),
                pltpu.VMEM((chips * lines, LANES), WIDE),
            ],
            heads=heads,
        )
        returned = exchange(head_partial, "group", same_core)
        copies = call(repeat, pltpu.VMEM((tensors, chips, lines, LANES), NARROW), (), (returned,))
        everyone = lax.all_to_all(copies, "tensor", 0, 0, tiled=True)
        out_hidden = call(
            finish,
            jax.ShapeDtypeStruct((sequences, width), NARROW),
            (core, slab_of),
            (everyone, hidden),
            [pltpu.VMEM((chips * lines, LANES), WIDE)],
            slab=slab,
        )
        return (
            out_hidden,
            new_keys.reshape(sequences, 1, head_dim),
            new_values.reshape(sequences, 1, head_dim),
        )

    in_specs = (
        P("group", None),
        P(),
        P(),
        P("group", "tensor"),
        P("group", "tensor"),
        P("group", "tensor"),
        P("tensor", "group"),
        P("group", "tensor", None, None),
        P("group", "tensor", None, None),
        P("group"),
    )
    out_specs = (P("group", None), P("group", "tensor", None), P("group", "tensor", None))
    return jax.shard_map(body, mesh=mesh, in_specs=in_specs, out_specs=out_specs, check_vma=False)
```

time: 99.9 us -> 85.7 us (0.86)
  blocking collectives: 0 us -> 74.3 us
  waiting for transfers between devices: 44.3 us -> 0.01 us
  starting transfers between devices: 29.5 us -> 1.1 us
  matrix products: 11 us -> 0 us
  Pallas kernels: 0 us -> 9.23 us
  other arithmetic: 7.43 us -> 0 us
  local copies, waits for them, and re-layouts: 6.07 us -> 0.03 us
    all_to_all x0 -> x5, blocking collectives: none -> 74.3 us  [the longest x4 61 us: exchange(): return lax.all_to_all(tiles, axis, 0, 0, tiled=True, axis_index_groups=sets)]
    all_to_all x5 -> x0, waiting for transfers between devices: 44.2 us -> none  [the longest x4 37.4 us: exchange(): return lax.all_to_all(tiles, axis, 0, 0, tiled=True, axis_index_groups=sets)]
    all_to_all x5 -> x0, starting transfers between devices: 28.7 us -> none  [the longest x4 22.2 us: exchange(): return lax.all_to_all(tiles, axis, 0, 0, tiled=True, axis_index_groups=sets)]
    dot_general x11 -> x0, matrix products: 11 us -> none  [the longest x3 3.24 us: project(): jnp.dot(own, w, preferred_element_type=jnp.float32)]
    pallas_call x0 -> x6, Pallas kernels: none -> 9.23 us  [call(): pl.pallas_call(functools.partial(kernel, **sizes), out_shape=outs, in_spe...]
    convert_element_type x6 -> x0, other arithmetic: 2.4 us -> none  [the longest x1 1.01 us: body(): (hidden_wide * lax.rsqrt(mean_square + 1e-05) * norm_gain).astype(jnp.bfl...]
    reshape x8 -> x0, local copies, waits for them, and re-layouts: 2.08 us -> none  [the longest x1 0.89 us: body(): partial = jnp.concatenate([project(w_query, other_query), project(w_key,...]
    broadcast_in_dim x3 -> x0, local copies, waits for them, and re-layouts: 1.66 us -> none  [the longest x1 0.85 us: body(): jnp.broadcast_to(returned[None], (tensors, *returned.shape))]
  transfers between devices with their start and end apart: 9 -> 4, of which waited for: 5 -> 0; matrix products, arithmetic and copies ran while one was open for 19% -> 0% of each run, Pallas kernels for 0% -> 2%
where the time goes in v2:
time: 85.7 us; the launch traced here: 85.4 us
  blocking collectives  74.3 us (87%)
  Pallas kernels  9.23 us (11%)
  starting transfers between devices  1.1 us (1%)
    all_to_all x4, blocking collectives, exchange(): return lax.all_to_all(tiles, axis, 0, 0, tiled=True, axis_index_groups=sets)  61 us
    all_to_all x1, blocking collectives, body(): everyone = lax.all_to_all(copies, 'tensor', 0, 0, tiled=True)  13.3 us
    pallas_call x6, Pallas kernels, call(): pl.pallas_call(functools.partial(kernel, **sizes), out_shape=outs, in_spe...  9.23 us
  transfers between devices with their start and end apart: 4, of which 0 were waited for; matrix products, arithmetic and copies ran while one was open for 0% of the time, Pallas kernels for 2%

profile of v2, /device:TPU:2, one launch (start us, length us, event | category | flops | bytes accessed | tf_op | source)
XLA Modules:
  0.0 85.4 jit_solution(16753260388960972695)
XLA Ops:
  0.6 0.1 collective-permute-start
  0.7 0.5 collective-permute-start.3
  1.2 0.1 collective-permute-start.1
  1.3 0.4 collective-permute-start.2
  1.7 1.7 %arrange.1 = (bf16[16,16,128]{2,1,0:T(8,128)(2,1)S(1)}, f32[2,128]{1,0:T(2,128)S(1)}, f32[2,128]{1,0:T(2,128)S(1)}, bf16[512,2048]{1,0:T(8,128)(2,1)S(1)}, bf16[...) custom-call(s32[1]{0:T(128)} %bitcast.core_ref, bf16[2,16384]{1,0:T(2,128)(2,1)} %hidden_ref.1, f32[1,16384]{1,0:T(1,128)} %bitcast.4, ...), custom_call_target="tpu_custom_call" | custom-call | tf_op jit(solution)/shard_map/arrange/pallas_call | solution.py:30
  3.5 17.8 %all_to_all.25.x_ref = bf16[16,16,128]{2,1,0:T(8,128)(2,1)S(1)} all-to-all(bf16[16,16,128]{2,1,0:T(8,128)(2,1)S(1)} %get-tuple-element.17), channel_id=1, replica_groups={{0,16,32,48,64,80,96,112,129,145,161,177,193,209,225,241},{1,17,33,49,6..., dimensions={0} | all-to-all | bytes 131072 | tf_op jit(solution)/shard_map/all_to_all | solution.py:205
  21.3 0.0 collective-permute-done.1.refs_3_
  21.3 0.0 collective-permute-done.2.refs_5_
  21.3 0.0 collective-permute-done.refs_1_
  21.3 0.0 collective-permute-done.3.other_ref
  21.3 0.0 copy-start
  21.3 0.0 copy-start.1
  21.4 0.0 copy-start.4
  21.4 2.7 %project.1 = f32[16,2,2304]{2,1,0:T(2,128)S(1)} custom-call(bf16[16,16,128]{2,1,0:T(8,128)(2,1)S(1)} %all_to_all.25.x_ref, bf16[512,2048]{1,0:T(8,128)(2,1)S(1)} %get-tuple-element.19.refs_0_, bf16[512,2048]{1,0:T(8,128)(2,1)} %collective-permute-done.refs_1_, bf16[512,128]{1,0:T(8,128)(2,1)S(1)} %get-tuple-element.21.refs_2_, ...), custom_call_target="tpu_custom_call" | custom-call | tf_op jit(solution)/shard_map/project/pallas_call | solution.py:30
  24.0 15.5 %all_to_all.26.part_ref = f32[16,2,2304]{2,1,0:T(2,128)S(1)} all-to-all(f32[16,2,2304]{2,1,0:T(2,128)S(1)} %project.1), channel_id=1, replica_groups={{0,16,32,48,64,80,96,112,128,144,160,176,192,208,224,240},{8,24,40,56,7..., dimensions={0} | all-to-all | bytes 589824 | tf_op jit(solution)/shard_map/all_to_all | solution.py:205
  39.5 0.0 copy-done
  39.5 0.0 copy-done.1
  39.5 0.0 copy-done.4
  39.5 0.0 copy-start.2
  39.5 2.6 %attend.1 = (bf16[16,32,128]{2,1,0:T(8,128)(2,1)S(1)}, bf16[2,128]{1,0:T(2,128)(2,1)}, bf16[2,128]{1,0:T(2,128)(2,1)}) custom-call(s32[2]{0:T(128)S(1)} %copy-done.4, f32[16,2,2304]{2,1,0:T(2,128)S(1)} %all_to_all.26.part_ref, f32[2,128]{1,0:T(2,128)S(1)} %get-tuple-element.25.cos_ref, f32[2,128]{1,0:T(2,128)S(1)} %get-tuple-element.26.sin_ref, ...), custom_call_target="tpu_custom_call" | custom-call | tf_op jit(solution)/shard_map/attend/pallas_call | solution.py:30
  42.1 14.6 %all_to_all.27.x_ref = bf16[16,32,128]{2,1,0:T(8,128)(2,1)S(1)} all-to-all(bf16[16,32,128]{2,1,0:T(8,128)(2,1)S(1)} %get-tuple-element.27), channel_id=1, replica_groups={{0,16,32,48,64,80,96,112,128,144,160,176,192,208,224,240},{8,24,40,56,7..., dimensions={0} | all-to-all | bytes 262144 | tf_op jit(solution)/shard_map/all_to_all | solution.py:205
  56.7 0.0 copy-done.2
  56.7 0.0 copy-start.3
  56.7 0.0 copy-start.5
  56.7 0.8 project_out.1
  57.5 13.1 %all_to_all.28.x_ref = bf16[16,16,128]{2,1,0:T(8,128)(2,1)S(1)} all-to-all(bf16[16,16,128]{2,1,0:T(8,128)(2,1)S(1)} %project_out.1), channel_id=1, replica_groups={{0,16,32,48,64,80,96,112,128,144,160,176,192,208,224,240},{8,24,40,56,7..., dimensions={0} | all-to-all | bytes 131072 | tf_op jit(solution)/shard_map/all_to_all | solution.py:205
  70.7 0.1 repeat.1
  70.8 13.3 %all_to_all.29.parts_ref = bf16[8,16,16,128]{3,2,1,0:T(8,128)(2,1)S(1)} all-to-all(bf16[8,16,16,128]{3,2,1,0:T(8,128)(2,1)S(1)} %repeat.1), channel_id=1, replica_groups=mesh['group'=32,'tensor'=8] {'tensor'}, dimensions={0} | all-to-all | bytes 1048576 | tf_op jit(solution)/shard_map/all_to_all | solution.py:301
  84.0 0.0 copy-done.3
  84.0 0.0 copy-done.5
  84.0 1.4 %finish.1 = bf16[2,16384]{1,0:T(2,128)(2,1)} custom-call(s32[1]{0:T(128)} %bitcast.core_ref, s32[32]{0:T(128)S(1)} %copy-done.5, bf16[8,16,16,128]{3,2,1,0:T(8,128)(2,1)S(1)} %all_to_all.29.parts_ref, bf16[2,16384]{1,0:T(2,128)(2,1)S(1)} %copy-done.3), custom_call_target="tpu_custom_call" | custom-call | tf_op jit(solution)/shard_map/finish/pallas_call | solution.py:30
Async XLA Ops:
  0.6 20.7 %collective-permute-start = (bf16[512,2048]{1,0:T(8,128)(2,1)}, bf16[512,2048]{1,0:T(8,128)(2,1)}, u32[]{:S(2)}, u32[]{:S(2)}) collective-permute-start(bf16[512,2048]{1,0:T(8,128)(2,1)} %refs_4_.1), channel_id=1, source_target_pairs={{0,8},{8,0},{16,24},{24,16},{32,40},{40,32},{48,56},{56,48},{64,72... | collective-permute-start | bytes 6291464 | tf_op jit(solution)/shard_map/ppermute | solution.py:235
  0.7 20.6 %collective-permute-start.3 = (bf16[2048,512]{1,0:T(8,128)(2,1)}, bf16[2048,512]{1,0:T(8,128)(2,1)S(1)}, u32[]{:S(2)}, u32[]{:S(2)}) collective-permute-start(bf16[2048,512]{1,0:T(8,128)(2,1)} %w_ref.1), channel_id=1, source_target_pairs={{0,8},{8,0},{16,24},{24,16},{32,40},{40,32},{48,56},{56,48},{64,72... | collective-permute-start | bytes 6291464 | tf_op jit(solution)/shard_map/ppermute | solution.py:235
  1.2 20.1 %collective-permute-start.1 = (bf16[512,128]{1,0:T(8,128)(2,1)}, bf16[512,128]{1,0:T(8,128)(2,1)S(1)}, u32[]{:S(2)}, u32[]{:S(2)}) collective-permute-start(bf16[512,128]{1,0:T(8,128)(2,1)} %refs_5_.1), channel_id=1, source_target_pairs={{0,8},{8,0},{16,24},{24,16},{32,40},{40,32},{48,56},{56,48},{64,72... | collective-permute-start | bytes 393224 | tf_op jit(solution)/shard_map/ppermute | solution.py:235
  1.3 20.0 %collective-permute-start.2 = (bf16[512,128]{1,0:T(8,128)(2,1)}, bf16[512,128]{1,0:T(8,128)(2,1)S(1)}, u32[]{:S(2)}, u32[]{:S(2)}) collective-permute-start(bf16[512,128]{1,0:T(8,128)(2,1)} %refs_6_.1), channel_id=1, source_target_pairs={{0,8},{8,0},{16,24},{24,16},{32,40},{40,32},{48,56},{56,48},{64,72... | collective-permute-start | bytes 393224 | tf_op jit(solution)/shard_map/ppermute | solution.py:235
  21.3 18.2 %copy-start = (bf16[2,1,4096,128]{3,2,1,0:T(8,128)(2,1)S(1)}, bf16[2,1,4096,128]{3,2,1,0:T(8,128)(2,1)}, u32[]{:S(2)}) copy-start(bf16[2,1,4096,128]{3,2,1,0:T(8,128)(2,1)} %k_ref.1) | copy-start | bytes 6291460
  21.3 18.2 %copy-start.1 = (bf16[2,1,4096,128]{3,2,1,0:T(8,128)(2,1)S(1)}, bf16[2,1,4096,128]{3,2,1,0:T(8,128)(2,1)}, u32[]{:S(2)}) copy-start(bf16[2,1,4096,128]{3,2,1,0:T(8,128)(2,1)} %v_ref.1) | copy-start | bytes 6291460
  21.4 18.2 %copy-start.4 = (s32[2]{0:T(128)S(1)}, s32[2]{0:T(128)}, u32[]{:S(2)}) copy-start(s32[2]{0:T(128)} %length_ref.1) | copy-start | bytes 28
  39.5 17.2 %copy-start.2 = (bf16[2048,512]{1,0:T(8,128)(2,1)S(1)}, bf16[2048,512]{1,0:T(8,128)(2,1)}, u32[]{:S(2)}) copy-start(bf16[2048,512]{1,0:T(8,128)(2,1)} %w_ref.1) | copy-start | bytes 6291460
  56.7 27.3 %copy-start.3 = (bf16[2,16384]{1,0:T(2,128)(2,1)S(1)}, bf16[2,16384]{1,0:T(2,128)(2,1)}, u32[]{:S(2)}) copy-start(bf16[2,16384]{1,0:T(2,128)(2,1)} %hidden_ref.1) | copy-start | bytes 196612
  56.7 27.3 %copy-start.5 = (s32[32]{0:T(128)S(1)}, s32[32]{0:T(128)}, u32[]{:S(2)}) copy-start(s32[32]{0:T(128)} %slab_ref.1) | copy-start | bytes 388

commit v3 on v2

--- a/solution.py
+++ b/solution.py
@@ -40,20 +40,32 @@
 
 def arrange(core_ref, *refs, slab):
     far, refs = refs[:7], refs[7:]
-    out_ref, cos_ref, sin_ref, *kept, slab_ref, length_ref, hidden_ref, gain_ref, rows_ref, sems = refs
-    near = (hidden_ref, gain_ref, slab_ref, length_ref, *kept)
+    out_ref, cos_ref, sin_ref, kept_ref, length_ref, slab_ref, hidden_ref, gain_ref, rows_ref, sems = refs
+    near = [length_ref, slab_ref, hidden_ref, gain_ref]
+    offset = 0
+    for weight in far[4:]:
+        near.append(kept_ref.at[:, offset : offset + weight.shape[1]])
+        offset += weight.shape[1]
     copies = [pltpu.make_async_copy(f, n, sems.at[i]) for i, (f, n) in enumerate(zip(far, near))]
     for copy in copies:
         copy.start()
-    copies, later = copies[:4], copies[4:]
     sequences, width = hidden_ref.shape
     head_dim = cos_ref.shape[1]
     core = core_ref[0]
-    lane = lax.broadcasted_iota(jnp.int32, (1, head_dim), 1)
+    lane = lax.broadcasted_iota(jnp.int32, (sequences, head_dim), 1)
     half_dim = head_dim // 2
     place_in_half = jnp.where(lane < half_dim, lane, lane - half_dim).astype(WIDE)
     frequency = jnp.exp(-math.log(ROTARY_BASE) * (2.0 * place_in_half) / head_dim)
-    for copy in copies:
+    copies[0].wait()
+    row = lax.broadcasted_iota(jnp.int32, (sequences, head_dim), 0)
+    position = jnp.full((sequences, head_dim), length_ref[0], jnp.int32)
+    for s in range(1, sequences):
+        position = jnp.where(row == s, length_ref[s], position)
+    angle = position.astype(WIDE) * frequency
+    sine = jnp.sin(angle)
+    cos_ref[...] = jnp.cos(angle)
+    sin_ref[...] = jnp.where(lane < half_dim, -sine, sine)
+    for copy in copies[1:4]:
         copy.wait()
     squares = jnp.zeros((sequences, slab), WIDE)
     for first in range(0, width, slab):
@@ -75,12 +87,7 @@
                 ]
     for chip in range(chips):
         out_ref[chip] = rows_ref[chip * lines : (chip + 1) * lines, :].astype(NARROW)
-    for s in range(sequences):
-        angle = length_ref[s].astype(WIDE) * frequency
-        cos_ref[s : s + 1, :] = jnp.cos(angle)
-        sine = jnp.sin(angle)
-        sin_ref[s : s + 1, :] = jnp.where(lane < half_dim, -sine, sine)
-    for copy in later:
+    for copy in copies[4:]:
         copy.wait()
 
 
@@ -94,21 +101,17 @@
     )
 
 
-def project(x_ref, *refs, chunk):
-    *weights, out_ref, wide_ref = refs
-    depth = weights[0].shape[0]
+def project(x_ref, w_ref, other_ref, out_ref, wide_ref, *, chunk):
+    depth, width = w_ref.shape
     x = rows_of(x_ref, wide_ref, 2 * depth // LANES)
     own, other = x[:, :depth], x[:, depth:]
-    rows = out_ref.shape[1]
-    offset = 0
-    for mine, partners in zip(weights[0::2], weights[1::2]):
-        step = min(chunk, mine.shape[1])
-        for first in range(0, mine.shape[1], step):
-            part = jnp.dot(own, mine[:, first : first + step], preferred_element_type=WIDE)
-            part += jnp.dot(other, partners[:, first : first + step], preferred_element_type=WIDE)
-            for chip in range(out_ref.shape[0]):
-                out_ref[chip, :, offset : offset + step] = part[chip * rows : (chip + 1) * rows]
-            offset += step
+    chips, rows = out_ref.shape[:2]
+    for first in range(0, width, chunk):
+        last = min(first + chunk, width)
+        part = jnp.dot(own, w_ref[:, first:last], preferred_element_type=WIDE)
+        part += jnp.dot(other, other_ref[:, first:last], preferred_element_type=WIDE)
+        for chip in range(chips):
+            out_ref[chip, :, first:last] = part[chip * rows : (chip + 1) * rows]
 
 
 def attend(
@@ -125,36 +128,50 @@
         for h in range(heads + 2):
             heads_ref[s, h : h + 1, :] = total[s : s + 1, h * head_dim : (h + 1) * head_dim]
     value_ref[...] = total[:, (heads + 1) * head_dim :].astype(NARROW)
-    new_keys = []
+    scaled, new_keys, own_scores = [], [], []
     for s in range(sequences):
         cosine, sine = cos_ref[s : s + 1], sin_ref[s : s + 1]
 
         def rotate(x):
             return x * cosine + pltpu.roll(x, head_dim // 2, 1) * sine
 
-        query = rotate(heads_ref[s, :heads, :])
-        scaled = (query / math.sqrt(head_dim)).astype(NARROW)
-        new_key = rotate(heads_ref[s, heads : heads + 1, :]).astype(NARROW)
+        query = (rotate(heads_ref[s, :heads, :]) / math.sqrt(head_dim)).astype(NARROW)
+        new_key = rotate(heads_ref[s, heads : heads + 1, :]).astype(NARROW).astype(WIDE)
+        scaled.append(query)
+        new_keys.append(new_key)
+        own_scores.append(jnp.sum(query.astype(WIDE) * new_key, axis=1, keepdims=True))
+    key_ref[...] = jnp.concatenate(new_keys, axis=0).astype(NARROW)
+    nothing = jnp.zeros((heads, head_dim), NARROW)
+    queries = jnp.concatenate(
+        [
+            jnp.concatenate([q if i == s else nothing for i in range(sequences)], axis=1)
+            for s, q in enumerate(scaled)
+        ],
+        axis=0,
+    )
+    keys = jnp.concatenate([k_ref[s, 0] for s in range(sequences)], axis=1)
+    scores = lax.dot_general(
+        queries, keys, (((1,), (1,)), ((), ())), preferred_element_type=WIDE
+    )
+    weights, own_weights = [], []
+    for s in range(sequences):
+        visible = lax.broadcasted_iota(jnp.int32, (heads, cached), 1) < length_ref[s]
+        masked = jnp.where(visible, scores[s * heads : (s + 1) * heads], -1e30)
+        highest = jnp.maximum(jnp.max(masked, axis=1, keepdims=True), own_scores[s])
+        exponent = jnp.where(visible, jnp.exp(masked - highest), 0.0)
+        own_exp = jnp.exp(own_scores[s] - highest)
+        share = 1.0 / (jnp.sum(exponent, axis=1, keepdims=True) + own_exp)
+        weights.append((exponent * share).astype(NARROW))
+        own_weights.append((own_exp * share).astype(NARROW))
+    values = jnp.concatenate([v_ref[s, 0] for s in range(sequences)], axis=1)
+    combined = jnp.dot(jnp.concatenate(weights, axis=0), values, preferred_element_type=WIDE)
+    for s in range(sequences):
         new_value = heads_ref[s, heads + 1 : heads + 2, :].astype(NARROW)
-        new_keys.append(new_key.astype(WIDE))
-        scores = lax.dot_general(
-            scaled, k_ref[s, 0], (((1,), (1,)), ((), ())), preferred_element_type=WIDE
-        )
-        own_score = jnp.sum(scaled.astype(WIDE) * new_key.astype(WIDE), axis=1, keepdims=True)
-        visible = lax.broadcasted_iota(jnp.int32, (heads, cached), 1) < length_ref[s]
-        masked = jnp.where(visible, scores, -1e30)
-        highest = jnp.maximum(jnp.max(masked, axis=1, keepdims=True), own_score)
-        exponent = jnp.where(visible, jnp.exp(masked - highest), 0.0)
-        own_exp = jnp.exp(own_score - highest)
-        share = 1.0 / (jnp.sum(exponent, axis=1, keepdims=True) + own_exp)
-        weights = (exponent * share).astype(NARROW)
-        own_weight = (own_exp * share).astype(NARROW)
-        combined = jnp.dot(weights, v_ref[s, 0], preferred_element_type=WIDE)
-        combined = combined + own_weight.astype(WIDE) * new_value.astype(WIDE)
-        attended = combined.astype(NARROW)
+        mixed = combined[s * heads : (s + 1) * heads, s * head_dim : (s + 1) * head_dim]
+        mixed = mixed + own_weights[s].astype(WIDE) * new_value.astype(WIDE)
+        attended = mixed.astype(NARROW)
         for target in range(out_ref.shape[0]):
             out_ref[target, s * heads : (s + 1) * heads, :] = attended
-    key_ref[...] = jnp.concatenate(new_keys, axis=0).astype(NARROW)
 
 
 def project_out(x_ref, w_ref, other_ref, out_ref, rows_ref, parts_ref, *, heads):
@@ -231,43 +248,39 @@
         heads = w_query.shape[1] // head_dim
         columns = w_query.shape[1] + w_key.shape[1] + w_value.shape[1]
         core = (lax.axis_index("group") % 2).reshape(1)
-        other_query, other_key, other_value, other_out = (
-            lax.ppermute(w, "group", partner) for w in (w_query, w_key, w_value, w_out)
-        )
+        other_out = lax.ppermute(w_out, "group", partner)
         lines = sequences * 2 * slab // LANES
-        arranged, cosine, sine, near_query, near_key, near_value = call(
+        arranged, cosine, sine, own_weights = call(
             arrange,
             (
                 pltpu.VMEM((chips, lines, LANES), NARROW),
                 pltpu.VMEM((sequences, head_dim), WIDE),
                 pltpu.VMEM((sequences, head_dim), WIDE),
-                *(pltpu.VMEM(w.shape, NARROW) for w in (w_query, w_key, w_value)),
+                pltpu.VMEM((slab, columns), NARROW),
             ),
             (core,),
             (),
             [
+                pltpu.SMEM((sequences,), jnp.int32),
                 pltpu.SMEM((groups,), jnp.int32),
-                pltpu.SMEM((sequences,), jnp.int32),
                 pltpu.VMEM((sequences, width), NARROW),
                 pltpu.VMEM((1, width), WIDE),
                 pltpu.VMEM((chips * lines, LANES), WIDE),
                 pltpu.SemaphoreType.DMA((7,)),
             ],
-            (hidden, norm_gain.reshape(1, width), slab_of, lengths, w_query, w_key, w_value),
+            (lengths, slab_of, hidden, norm_gain.reshape(1, width), w_query, w_key, w_value),
             slab=slab,
         )
+        other_weights = lax.ppermute(own_weights, "group", partner)
         features = exchange(arranged, ("group", "tensor"), near)
-        features, other_query, other_key, other_value, other_out = lax.optimization_barrier(
-            (features, other_query, other_key, other_value, other_out)
+        features, other_weights, other_out = lax.optimization_barrier(
+            (features, other_weights, other_out)
         )
         partial = call(
             project,
             pltpu.VMEM((chips, sequences, columns), WIDE),
             (),
-            (
-                features,
-                near_query, *in_vmem(other_query), near_key, *in_vmem(other_key), near_value, *in_vmem(other_value),
-            ),
+            (features, own_weights, *in_vmem(other_weights)),
             [pltpu.VMEM((chips * lines, LANES), WIDE)],
             chunk=512,
         )
@@ -296,7 +309,7 @@
             ],
             heads=heads,
         )
-        returned = exchange(head_partial, "group", same_core)
+        returned = exchange(head_partial, ("group", "tensor"), near)
         copies = call(repeat, pltpu.VMEM((tensors, chips, lines, LANES), NARROW), (), (returned,))
         everyone = lax.all_to_all(copies, "tensor", 0, 0, tiled=True)
         out_hidden = call(

time: 85.7 us -> 83.1 us (0.970)
  Pallas kernels: 9.23 us -> 7.39 us
  starting transfers between devices: 1.1 us -> 0.23 us
    pallas_call x6, Pallas kernels: 9.23 us -> 7.39 us  [call(): pl.pallas_call(functools.partial(kernel, **sizes), out_shape=outs, in_spe...]
    all_to_all x4, blocking collectives: 61 us -> 59.8 us  [exchange(): return lax.all_to_all(tiles, axis, 0, 0, tiled=True, axis_index_groups=sets)]
    all_to_all x1, blocking collectives: 13.3 us -> 14.3 us  [body(): everyone = lax.all_to_all(copies, 'tensor', 0, 0, tiled=True)]
    ppermute x4 -> x2, starting transfers between devices: 1.1 us -> 0.23 us  [the longest x1 0.14 us: body(): other_out = lax.ppermute(w_out, 'group', partner)]
  transfers between devices with their start and end apart: 4 -> 2, of which waited for: 0 -> 0; matrix products, arithmetic and copies ran while one was open for 0% -> 0% of each run, Pallas kernels for 2% -> 0%
where the time goes in v3:
time: 83.1 us; the launch traced here: 82.9 us
  blocking collectives  74.1 us (89%)
  Pallas kernels  7.39 us (9%)
    all_to_all x4, blocking collectives, exchange(): return lax.all_to_all(tiles, axis, 0, 0, tiled=True, axis_index_groups=sets)  59.8 us
    all_to_all x1, blocking collectives, body(): everyone = lax.all_to_all(copies, 'tensor', 0, 0, tiled=True)  14.3 us
    pallas_call x6, Pallas kernels, call(): pl.pallas_call(functools.partial(kernel, **sizes), out_shape=outs, in_spe...  7.39 us
  transfers between devices with their start and end apart: 2, of which 0 were waited for; matrix products, arithmetic and copies ran while one was open for 0% of the time, Pallas kernels for 0%

profile of v3, /device:TPU:2, one launch (start us, length us, event | category | flops | bytes accessed | tf_op | source)
XLA Modules:
  0.0 82.9 jit_solution(14757883539081532435)
XLA Ops:
  0.6 0.0 copy-start.2
  0.7 1.9 %arrange.1 = (bf16[16,16,128]{2,1,0:T(8,128)(2,1)S(1)}, f32[2,128]{1,0:T(2,128)S(1)}, f32[2,128]{1,0:T(2,128)S(1)}, bf16[512,2304]{1,0:T(8,128)(2,1)S(1)}) custom-call(s32[1]{0:T(128)} %bitcast.core_ref, s32[2]{0:T(128)} %length_ref.1, s32[32]{0:T(128)} %slab_ref.1, bf16[2,16384]{1,0:T(2,128)(2,1)} %hidden_ref.1, f32[1,16384]{1,0:T(1,128)} %bitcast.4, ...), custom_call_target="tpu_custom_call" | custom-call | tf_op jit(solution)/shard_map/arrange/pallas_call | solution.py:30
  2.5 0.1 collective-permute-start
  2.6 0.4 copy-done.2
  3.0 0.1 collective-permute-start.1
  3.1 17.8 %all_to_all.25.x_ref = bf16[16,16,128]{2,1,0:T(8,128)(2,1)S(1)} all-to-all(bf16[16,16,128]{2,1,0:T(8,128)(2,1)S(1)} %get-tuple-element.13), channel_id=1, replica_groups={{0,16,32,48,64,80,96,112,129,145,161,177,193,209,225,241},{1,17,33,49,6..., dimensions={0} | all-to-all | bytes 131072 | tf_op jit(solution)/shard_map/all_to_all | solution.py:222
  20.9 0.0 copy-start
  20.9 0.0 copy-start.1
  20.9 0.0 copy-start.4
  20.9 0.0 collective-permute-done.1.other_ref
  21.0 0.0 collective-permute-done.other_ref
  21.0 0.9 %project.1 = f32[16,2,2304]{2,1,0:T(2,128)S(1)} custom-call(bf16[16,16,128]{2,1,0:T(8,128)(2,1)S(1)} %all_to_all.25.x_ref, bf16[512,2304]{1,0:T(8,128)(2,1)S(1)} %get-tuple-element.14.w_ref, bf16[512,2304]{1,0:T(8,128)(2,1)S(1)} %collective-permute-done.other_ref), custom_call_target="tpu_custom_call" | custom-call | tf_op jit(solution)/shard_map/project/pallas_call | solution.py:30
  21.9 15.9 %all_to_all.26.part_ref = f32[16,2,2304]{2,1,0:T(2,128)S(1)} all-to-all(f32[16,2,2304]{2,1,0:T(2,128)S(1)} %project.1), channel_id=1, replica_groups={{0,16,32,48,64,80,96,112,128,144,160,176,192,208,224,240},{8,24,40,56,7..., dimensions={0} | all-to-all | bytes 589824 | tf_op jit(solution)/shard_map/all_to_all | solution.py:222
  37.8 0.0 copy-done
  37.8 0.0 copy-done.1
  37.8 0.0 copy-done.4
  37.8 2.4 %attend.1 = (bf16[16,32,128]{2,1,0:T(8,128)(2,1)S(1)}, bf16[2,128]{1,0:T(2,128)(2,1)}, bf16[2,128]{1,0:T(2,128)(2,1)}) custom-call(s32[2]{0:T(128)S(1)} %copy-done.4, f32[16,2,2304]{2,1,0:T(2,128)S(1)} %all_to_all.26.part_ref, f32[2,128]{1,0:T(2,128)S(1)} %get-tuple-element.17.cos_ref, f32[2,128]{1,0:T(2,128)S(1)} %get-tuple-element.18.sin_ref, ...), custom_call_target="tpu_custom_call" | custom-call | tf_op jit(solution)/shard_map/attend/pallas_call | solution.py:30
  40.1 14.6 %all_to_all.27.x_ref = bf16[16,32,128]{2,1,0:T(8,128)(2,1)S(1)} all-to-all(bf16[16,32,128]{2,1,0:T(8,128)(2,1)S(1)} %get-tuple-element.19), channel_id=1, replica_groups={{0,16,32,48,64,80,96,112,128,144,160,176,192,208,224,240},{8,24,40,56,7..., dimensions={0} | all-to-all | bytes 262144 | tf_op jit(solution)/shard_map/all_to_all | solution.py:222
  54.7 0.0 copy-start.3
  54.7 0.0 copy-start.5
  54.7 0.8 project_out.1
  55.6 11.5 %all_to_all.28.x_ref = bf16[16,16,128]{2,1,0:T(8,128)(2,1)S(1)} all-to-all(bf16[16,16,128]{2,1,0:T(8,128)(2,1)S(1)} %project_out.1), channel_id=1, replica_groups={{0,16,32,48,64,80,96,112,129,145,161,177,193,209,225,241},{1,17,33,49,6..., dimensions={0} | all-to-all | bytes 131072 | tf_op jit(solution)/shard_map/all_to_all | solution.py:222
  67.1 0.1 repeat.1
  67.2 14.3 %all_to_all.29.parts_ref = bf16[8,16,16,128]{3,2,1,0:T(8,128)(2,1)S(1)} all-to-all(bf16[8,16,16,128]{3,2,1,0:T(8,128)(2,1)S(1)} %repeat.1), channel_id=1, replica_groups=mesh['group'=32,'tensor'=8] {'tensor'}, dimensions={0} | all-to-all | bytes 1048576 | tf_op jit(solution)/shard_map/all_to_all | solution.py:314
  81.5 0.0 copy-done.3
  81.5 0.0 copy-done.5
  81.5 1.4 %finish.1 = bf16[2,16384]{1,0:T(2,128)(2,1)} custom-call(s32[1]{0:T(128)} %bitcast.core_ref, s32[32]{0:T(128)S(1)} %copy-done.5, bf16[8,16,16,128]{3,2,1,0:T(8,128)(2,1)S(1)} %all_to_all.29.parts_ref, bf16[2,16384]{1,0:T(2,128)(2,1)S(1)} %copy-done.3), custom_call_target="tpu_custom_call" | custom-call | tf_op jit(solution)/shard_map/finish/pallas_call | solution.py:30
Async XLA Ops:
  0.6 2.4 %copy-start.2 = (bf16[2048,512]{1,0:T(8,128)(2,1)S(1)}, bf16[2048,512]{1,0:T(8,128)(2,1)}, u32[]{:S(2)}) copy-start(bf16[2048,512]{1,0:T(8,128)(2,1)} %w_ref.1) | copy-start | bytes 6291460
  2.5 18.4 %collective-permute-start = (bf16[512,2304]{1,0:T(8,128)(2,1)S(1)}, bf16[512,2304]{1,0:T(8,128)(2,1)S(1)}, u32[]{:S(2)}, u32[]{:S(2)}) collective-permute-start(bf16[512,2304]{1,0:T(8,128)(2,1)S(1)} %get-tuple-element.14.w_ref), channel_id=1, source_target_pairs={{0,8},{8,0},{16,24},{24,16},{32,40},{40,32},{48,56},{56,48},{64,72... | collective-permute-start | bytes 7077896 | tf_op jit(solution)/shard_map/ppermute | solution.py:274
  3.0 18.0 %collective-permute-start.1 = (bf16[2048,512]{1,0:T(8,128)(2,1)S(1)}, bf16[2048,512]{1,0:T(8,128)(2,1)S(1)}, u32[]{:S(2)}, u32[]{:S(2)}) collective-permute-start(bf16[2048,512]{1,0:T(8,128)(2,1)S(1)} %copy-done.2), channel_id=1, source_target_pairs={{0,8},{8,0},{16,24},{24,16},{32,40},{40,32},{48,56},{56,48},{64,72... | collective-permute-start | bytes 6291464 | tf_op jit(solution)/shard_map/ppermute | solution.py:251
  20.9 16.8 %copy-start = (bf16[2,1,4096,128]{3,2,1,0:T(8,128)(2,1)S(1)}, bf16[2,1,4096,128]{3,2,1,0:T(8,128)(2,1)}, u32[]{:S(2)}) copy-start(bf16[2,1,4096,128]{3,2,1,0:T(8,128)(2,1)} %k_ref.1) | copy-start | bytes 6291460
  20.9 16.8 %copy-start.1 = (bf16[2,1,4096,128]{3,2,1,0:T(8,128)(2,1)S(1)}, bf16[2,1,4096,128]{3,2,1,0:T(8,128)(2,1)}, u32[]{:S(2)}) copy-start(bf16[2,1,4096,128]{3,2,1,0:T(8,128)(2,1)} %v_ref.1) | copy-start | bytes 6291460
  20.9 16.8 %copy-start.4 = (s32[2]{0:T(128)S(1)}, s32[2]{0:T(128)}, u32[]{:S(2)}) copy-start(s32[2]{0:T(128)} %length_ref.1) | copy-start | bytes 28
  54.7 26.7 %copy-start.3 = (bf16[2,16384]{1,0:T(2,128)(2,1)S(1)}, bf16[2,16384]{1,0:T(2,128)(2,1)}, u32[]{:S(2)}) copy-start(bf16[2,16384]{1,0:T(2,128)(2,1)} %hidden_ref.1) | copy-start | bytes 196612
  54.7 26.7 %copy-start.5 = (s32[32]{0:T(128)S(1)}, s32[32]{0:T(128)}, u32[]{:S(2)}) copy-start(s32[32]{0:T(128)} %slab_ref.1) | copy-start | bytes 388

commit v4 on v3

--- a/solution.py
+++ b/solution.py
@@ -31,27 +31,45 @@
         functools.partial(kernel, **sizes),
         out_shape=outs,
         in_specs=at(pltpu.SMEM, scalars) + at(pltpu.HBM, far) + at(pltpu.VMEM, arrays),
-        out_specs=jax.tree.map(lambda _: pl.BlockSpec(memory_space=pltpu.VMEM), outs),
+        out_specs=jax.tree.map(
+            lambda out: pl.BlockSpec(
+                memory_space=pltpu.SMEM if out.dtype == jnp.int32 else pltpu.VMEM
+            ),
+            outs,
+        ),
         scratch_shapes=list(scratch),
         compiler_params=pltpu.CompilerParams(vmem_limit_bytes=8 * 1024 * 1024),
         name=kernel.__name__,
     )(*scalars, *in_hbm(*far), *arrays)
 
 
-def arrange(core_ref, *refs, slab):
-    far, refs = refs[:7], refs[7:]
-    out_ref, cos_ref, sin_ref, kept_ref, length_ref, slab_ref, hidden_ref, gain_ref, rows_ref, sems = refs
+def own_core():
+    return lax.rem(lax.axis_index("group"), 2)
+
+
+def arrange(*refs, slab):
+    far, refs = refs[:8], refs[8:]
+    (
+        out_ref, cos_ref, sin_ref, kept_ref, length_ref, slab_ref, hidden_ref, gain_ref, rows_ref, sems
+    ) = refs
     near = [length_ref, slab_ref, hidden_ref, gain_ref]
+    far = list(far)
     offset = 0
+    w_out = far.pop()
     for weight in far[4:]:
         near.append(kept_ref.at[:, offset : offset + weight.shape[1]])
         offset += weight.shape[1]
+    depth, columns = kept_ref.shape[0], w_out.shape[1]
+    for first in range(0, w_out.shape[0], depth):
+        far.append(w_out.at[first : first + depth, :])
+        near.append(kept_ref.at[:, offset : offset + columns])
+        offset += columns
     copies = [pltpu.make_async_copy(f, n, sems.at[i]) for i, (f, n) in enumerate(zip(far, near))]
     for copy in copies:
         copy.start()
     sequences, width = hidden_ref.shape
     head_dim = cos_ref.shape[1]
-    core = core_ref[0]
+    core = own_core()
     lane = lax.broadcasted_iota(jnp.int32, (sequences, head_dim), 1)
     half_dim = head_dim // 2
     place_in_half = jnp.where(lane < half_dim, lane, lane - half_dim).astype(WIDE)
@@ -102,7 +120,7 @@
 
 
 def project(x_ref, w_ref, other_ref, out_ref, wide_ref, *, chunk):
-    depth, width = w_ref.shape
+    depth, width = w_ref.shape[0], out_ref.shape[2]
     x = rows_of(x_ref, wide_ref, 2 * depth // LANES)
     own, other = x[:, :depth], x[:, depth:]
     chips, rows = out_ref.shape[:2]
@@ -174,14 +192,22 @@
             out_ref[target, s * heads : (s + 1) * heads, :] = attended
 
 
-def project_out(x_ref, w_ref, other_ref, out_ref, rows_ref, parts_ref, *, heads):
+def project_out(x_ref, w_ref, other_ref, out_ref, rows_ref, parts_ref, *, heads, slab):
     chips, lines = out_ref.shape[:2]
     x = rows_of(x_ref, rows_ref, heads)
-    rows = x.shape[0]
-    slab = w_ref.shape[1]
+    rows, inner = x.shape
+    depth, width = w_ref.shape
+    offset = width - inner // depth * slab
     pieces = slab // LANES
     for place, w in enumerate((w_ref, other_ref)):
-        part = jnp.dot(x, w[...], preferred_element_type=WIDE)
+        part = jnp.zeros((rows, slab), WIDE)
+        for block in range(inner // depth):
+            at = offset + block * slab
+            part += jnp.dot(
+                x[:, block * depth : (block + 1) * depth],
+                w[:, at : at + slab],
+                preferred_element_type=WIDE,
+            )
         for piece in range(pieces):
             parts_ref[pl.ds(place * pieces + piece, rows, stride=2 * pieces), :] = part[
                 :, piece * LANES : (piece + 1) * LANES
@@ -197,8 +223,12 @@
             out_ref[target, chip] = x
 
 
-def finish(core_ref, slab_ref, parts_ref, hidden_ref, out_ref, sums_ref, *, slab):
-    core = core_ref[0]
+def finish(
+    slab_ref, parts_ref, hidden_ref, key_in, value_in, out_ref, key_ref, value_ref, sums_ref, *, slab
+):
+    key_ref[...] = key_in[...]
+    value_ref[...] = value_in[...]
+    core = own_core()
     chips, lines = parts_ref.shape[1:3]
     sequences = hidden_ref.shape[0]
     pieces = slab // LANES
@@ -247,40 +277,38 @@
         head_dim = k_cache.shape[3]
         heads = w_query.shape[1] // head_dim
         columns = w_query.shape[1] + w_key.shape[1] + w_value.shape[1]
-        core = (lax.axis_index("group") % 2).reshape(1)
-        other_out = lax.ppermute(w_out, "group", partner)
         lines = sequences * 2 * slab // LANES
-        arranged, cosine, sine, own_weights = call(
+        kept = columns + w_out.shape[0] // slab * slab
+        arranged, cosine, sine, own_weights, near_lengths, near_slabs = call(
             arrange,
             (
                 pltpu.VMEM((chips, lines, LANES), NARROW),
                 pltpu.VMEM((sequences, head_dim), WIDE),
                 pltpu.VMEM((sequences, head_dim), WIDE),
-                pltpu.VMEM((slab, columns), NARROW),
+                pltpu.VMEM((slab, kept), NARROW),
+                pltpu.SMEM((sequences,), jnp.int32),
+                pltpu.SMEM((groups,), jnp.int32),
             ),
-            (core,),
+            (),
             (),
             [
-                pltpu.SMEM((sequences,), jnp.int32),
-                pltpu.SMEM((groups,), jnp.int32),
                 pltpu.VMEM((sequences, width), NARROW),
                 pltpu.VMEM((1, width), WIDE),
                 pltpu.VMEM((chips * lines, LANES), WIDE),
-                pltpu.SemaphoreType.DMA((7,)),
+                pltpu.SemaphoreType.DMA((7 + w_out.shape[0] // slab,)),
             ],
-            (lengths, slab_of, hidden, norm_gain.reshape(1, width), w_query, w_key, w_value),
+            (lengths, slab_of, hidden, norm_gain.reshape(1, width), w_query, w_key, w_value, w_out),
             slab=slab,
         )
         other_weights = lax.ppermute(own_weights, "group", partner)
         features = exchange(arranged, ("group", "tensor"), near)
-        features, other_weights, other_out = lax.optimization_barrier(
-            (features, other_weights, other_out)
-        )
+        features, other_weights = lax.optimization_barrier((features, other_weights))
+        other_weights, = in_vmem(other_weights)
         partial = call(
             project,
             pltpu.VMEM((chips, sequences, columns), WIDE),
             (),
-            (features, own_weights, *in_vmem(other_weights)),
+            (features, own_weights, other_weights),
             [pltpu.VMEM((chips * lines, LANES), WIDE)],
             chunk=512,
         )
@@ -289,10 +317,10 @@
             attend,
             (
                 pltpu.VMEM((chips, sequences * heads, head_dim), NARROW),
-                jax.ShapeDtypeStruct((sequences, head_dim), NARROW),
-                jax.ShapeDtypeStruct((sequences, head_dim), NARROW),
+                pltpu.VMEM((sequences, head_dim), NARROW),
+                pltpu.VMEM((sequences, head_dim), NARROW),
             ),
-            (lengths,),
+            (near_lengths,),
             (parts, cosine, sine, *in_vmem(k_cache, v_cache)),
             [pltpu.VMEM((sequences, heads + 8, head_dim), WIDE)],
             heads=heads,
@@ -302,21 +330,26 @@
             project_out,
             pltpu.VMEM((chips, lines, LANES), NARROW),
             (),
-            (gathered, *in_vmem(w_out, other_out)),
+            (gathered, own_weights, other_weights),
             [
                 pltpu.VMEM((chips * sequences * heads, head_dim), WIDE),
                 pltpu.VMEM((chips * lines, LANES), WIDE),
             ],
             heads=heads,
+            slab=slab,
         )
         returned = exchange(head_partial, ("group", "tensor"), near)
         copies = call(repeat, pltpu.VMEM((tensors, chips, lines, LANES), NARROW), (), (returned,))
         everyone = lax.all_to_all(copies, "tensor", 0, 0, tiled=True)
-        out_hidden = call(
+        out_hidden, new_keys, new_values = call(
             finish,
-            jax.ShapeDtypeStruct((sequences, width), NARROW),
-            (core, slab_of),
-            (everyone, hidden),
+            (
+                jax.ShapeDtypeStruct((sequences, width), NARROW),
+                jax.ShapeDtypeStruct((sequences, head_dim), NARROW),
+                jax.ShapeDtypeStruct((sequences, head_dim), NARROW),
+            ),
+            (near_slabs,),
+            (everyone, hidden, new_keys, new_values),
             [pltpu.VMEM((chips * lines, LANES), WIDE)],
             slab=slab,
         )

time: 83.1 us -> 81.8 us (0.984)
  Pallas kernels: 7.39 us -> 6.45 us
    pallas_call x6, Pallas kernels: 7.39 us -> 6.45 us  [call(): pl.pallas_call(functools.partial(kernel, **sizes), out_shape=outs, in_spe...]
  transfers between devices with their start and end apart: 2 -> 1, of which waited for: 0 -> 0; matrix products, arithmetic and copies ran while one was open for 0% -> 0% of each run, Pallas kernels for 0% -> 0%
where the time goes in v4:
time: 81.8 us; the launch traced here: 81.5 us
  blocking collectives  74.3 us (91%)
  Pallas kernels  6.45 us (8%)
    all_to_all x4, blocking collectives, exchange(): return lax.all_to_all(tiles, axis, 0, 0, tiled=True, axis_index_groups=sets)  59.8 us
    all_to_all x1, blocking collectives, body(): everyone = lax.all_to_all(copies, 'tensor', 0, 0, tiled=True)  14.4 us
    pallas_call x6, Pallas kernels, call(): pl.pallas_call(functools.partial(kernel, **sizes), out_shape=outs, in_spe...  6.45 us
  transfers between devices with their start and end apart: 1, of which 0 were waited for; matrix products, arithmetic and copies ran while one was open for 0% of the time, Pallas kernels for 0%

profile of v4, /device:TPU:2, one launch (start us, length us, event | category | flops | bytes accessed | tf_op | source)
XLA Modules:
  0.0 81.5 jit_solution(5482267743022664146)
XLA Ops:
  0.6 2.4 %arrange.1 = (bf16[16,16,128]{2,1,0:T(8,128)(2,1)S(1)}, f32[2,128]{1,0:T(2,128)S(1)}, f32[2,128]{1,0:T(2,128)S(1)}, bf16[512,4352]{1,0:T(8,128)(2,1)S(1)}, s32[2]{0:T(128)S(4)}, /*index=5*/s32[32]{0:T(128)S(4)}) custom-call(s32[2]{0:T(128)} %refs_0_.1, s32[32]{0:T(128)} %refs_1_.1, bf16[2,16384]{1,0:T(2,128)(2,1)} %hidden_ref.1, f32[1,16384]{1,0:T(1,128)} %bitcast.3, ...), custom_call_target="tpu_custom_call" | custom-call | tf_op jit(solution)/shard_map/arrange/pallas_call | solution.py:30
  3.0 0.1 collective-permute-start
  3.1 17.8 %all_to_all.25.x_ref = bf16[16,16,128]{2,1,0:T(8,128)(2,1)S(1)} all-to-all(bf16[16,16,128]{2,1,0:T(8,128)(2,1)S(1)} %get-tuple-element.19), channel_id=1, replica_groups={{0,16,32,48,64,80,96,112,129,145,161,177,193,209,225,241},{1,17,33,49,6..., dimensions={0} | all-to-all | bytes 131072 | tf_op jit(solution)/shard_map/all_to_all | solution.py:252
  21.0 0.0 copy-start
  21.0 0.0 copy-start.1
  21.0 0.0 collective-permute-done.other_ref
  21.0 0.9 %project.1 = f32[16,2,2304]{2,1,0:T(2,128)S(1)} custom-call(bf16[16,16,128]{2,1,0:T(8,128)(2,1)S(1)} %all_to_all.25.x_ref, bf16[512,4352]{1,0:T(8,128)(2,1)S(1)} %get-tuple-element.20.w_ref, bf16[512,4352]{1,0:T(8,128)(2,1)S(1)} %collective-permute-done.other_ref), custom_call_target="tpu_custom_call" | custom-call | tf_op jit(solution)/shard_map/project/pallas_call | solution.py:30
  21.9 16.0 %all_to_all.26.part_ref = f32[16,2,2304]{2,1,0:T(2,128)S(1)} all-to-all(f32[16,2,2304]{2,1,0:T(2,128)S(1)} %project.1), channel_id=1, replica_groups={{0,16,32,48,64,80,96,112,128,144,160,176,192,208,224,240},{8,24,40,56,7..., dimensions={0} | all-to-all | bytes 589824 | tf_op jit(solution)/shard_map/all_to_all | solution.py:252
  37.9 0.0 copy-done
  37.9 0.0 copy-done.1
  37.9 1.4 %attend.1 = (bf16[16,32,128]{2,1,0:T(8,128)(2,1)S(1)}, bf16[2,128]{1,0:T(2,128)(2,1)S(1)}, bf16[2,128]{1,0:T(2,128)(2,1)S(1)}) custom-call(s32[2]{0:T(128)S(4)} %get-tuple-element.18.length_ref, f32[16,2,2304]{2,1,0:T(2,128)S(1)} %all_to_all.26.part_ref, f32[2,128]{1,0:T(2,128)S(1)} %get-tuple-element.23.cos_ref, f32[2,128]{1,0:T(2,128)S(1)} %get-tuple-element.24.sin_ref, ...), custom_call_target="tpu_custom_call" | custom-call | tf_op jit(solution)/shard_map/attend/pallas_call | solution.py:30
  39.3 14.6 %all_to_all.27.x_ref = bf16[16,32,128]{2,1,0:T(8,128)(2,1)S(1)} all-to-all(bf16[16,32,128]{2,1,0:T(8,128)(2,1)S(1)} %get-tuple-element.25), channel_id=1, replica_groups={{0,16,32,48,64,80,96,112,128,144,160,176,192,208,224,240},{8,24,40,56,7..., dimensions={0} | all-to-all | bytes 262144 | tf_op jit(solution)/shard_map/all_to_all | solution.py:252
  53.9 0.0 copy-start.2
  53.9 0.8 project_out.1
  54.8 11.4 %all_to_all.28.x_ref = bf16[16,16,128]{2,1,0:T(8,128)(2,1)S(1)} all-to-all(bf16[16,16,128]{2,1,0:T(8,128)(2,1)S(1)} %project_out.1), channel_id=1, replica_groups={{0,16,32,48,64,80,96,112,129,145,161,177,193,209,225,241},{1,17,33,49,6..., dimensions={0} | all-to-all | bytes 131072 | tf_op jit(solution)/shard_map/all_to_all | solution.py:252
  66.2 0.1 repeat.1
  66.2 14.4 %all_to_all.29.parts_ref = bf16[8,16,16,128]{3,2,1,0:T(8,128)(2,1)S(1)} all-to-all(bf16[8,16,16,128]{3,2,1,0:T(8,128)(2,1)S(1)} %repeat.1), channel_id=1, replica_groups=mesh['group'=32,'tensor'=8] {'tensor'}, dimensions={0} | all-to-all | bytes 1048576 | tf_op jit(solution)/shard_map/all_to_all | solution.py:343
  80.7 0.0 copy-done.2
  80.7 0.8 %finish.1 = (bf16[2,16384]{1,0:T(2,128)(2,1)}, bf16[2,128]{1,0:T(2,128)(2,1)}, bf16[2,128]{1,0:T(2,128)(2,1)}) custom-call(s32[32]{0:T(128)S(4)} %get-tuple-element.17.slab_ref, bf16[8,16,16,128]{3,2,1,0:T(8,128)(2,1)S(1)} %all_to_all.29.parts_ref, bf16[2,16384]{1,0:T(2,128)(2,1)S(1)} %copy-done.2, bf16[2,128]{1,0:T(2,128)(2,1)S(1)} %get-tuple-element.26.key_in, ...), custom_call_target="tpu_custom_call" | custom-call | tf_op jit(solution)/shard_map/finish/pallas_call | solution.py:30
Async XLA Ops:
  3.0 17.9 %collective-permute-start = (bf16[512,4352]{1,0:T(8,128)(2,1)S(1)}, bf16[512,4352]{1,0:T(8,128)(2,1)S(1)}, u32[]{:S(2)}, u32[]{:S(2)}) collective-permute-start(bf16[512,4352]{1,0:T(8,128)(2,1)S(1)} %get-tuple-element.20.w_ref), channel_id=1, source_target_pairs={{0,8},{8,0},{16,24},{24,16},{32,40},{40,32},{48,56},{56,48},{64,72... | collective-permute-start | bytes 13369352 | tf_op jit(solution)/shard_map/ppermute | solution.py:303
  21.0 16.9 %copy-start = (bf16[2,1,4096,128]{3,2,1,0:T(8,128)(2,1)S(1)}, bf16[2,1,4096,128]{3,2,1,0:T(8,128)(2,1)}, u32[]{:S(2)}) copy-start(bf16[2,1,4096,128]{3,2,1,0:T(8,128)(2,1)} %k_ref.1) | copy-start | bytes 6291460
  21.0 16.9 %copy-start.1 = (bf16[2,1,4096,128]{3,2,1,0:T(8,128)(2,1)S(1)}, bf16[2,1,4096,128]{3,2,1,0:T(8,128)(2,1)}, u32[]{:S(2)}) copy-start(bf16[2,1,4096,128]{3,2,1,0:T(8,128)(2,1)} %v_ref.1) | copy-start | bytes 6291460
  53.9 26.7 %copy-start.2 = (bf16[2,16384]{1,0:T(2,128)(2,1)S(1)}, bf16[2,16384]{1,0:T(2,128)(2,1)}, u32[]{:S(2)}) copy-start(bf16[2,16384]{1,0:T(2,128)(2,1)} %hidden_ref.1) | copy-start | bytes 196612

commit v5 on v4

--- a/solution.py
+++ b/solution.py
@@ -109,13 +109,27 @@
         copy.wait()
 
 
-def rows_of(x_ref, wide_ref, pieces):
+def rows_of(x_ref, wide_ref, pieces, by_sequence=False):
     sources, lines = x_ref.shape[:2]
     for source in range(sources):
         wide_ref[source * lines : (source + 1) * lines, :] = x_ref[source].astype(WIDE)
-    rows = sources * lines // pieces
+    sequences = lines // pieces
+    if by_sequence:
+        starts, rows, stride = [s * pieces for s in range(sequences)], sources, lines
+    else:
+        starts, rows, stride = [0], sources * sequences, pieces
     return jnp.concatenate(
-        [wide_ref[pl.ds(p, rows, stride=pieces), :].astype(NARROW) for p in range(pieces)], axis=1
+        [
+            jnp.concatenate(
+                [
+                    wide_ref[pl.ds(start + p, rows, stride=stride), :].astype(NARROW)
+                    for p in range(pieces)
+                ],
+                axis=1,
+            )
+            for start in starts
+        ],
+        axis=0,
     )
 
 
@@ -176,7 +190,7 @@
         visible = lax.broadcasted_iota(jnp.int32, (heads, cached), 1) < length_ref[s]
         masked = jnp.where(visible, scores[s * heads : (s + 1) * heads], -1e30)
         highest = jnp.maximum(jnp.max(masked, axis=1, keepdims=True), own_scores[s])
-        exponent = jnp.where(visible, jnp.exp(masked - highest), 0.0)
+        exponent = jnp.exp(masked - highest)
         own_exp = jnp.exp(own_scores[s] - highest)
         share = 1.0 / (jnp.sum(exponent, axis=1, keepdims=True) + own_exp)
         weights.append((exponent * share).astype(NARROW))
@@ -193,12 +207,14 @@
 
 
 def project_out(x_ref, w_ref, other_ref, out_ref, rows_ref, parts_ref, *, heads, slab):
-    chips, lines = out_ref.shape[:2]
-    x = rows_of(x_ref, rows_ref, heads)
+    chips = x_ref.shape[0]
+    tiles, lines = out_ref.shape[:2]
+    x = rows_of(x_ref, rows_ref, heads, by_sequence=True)
     rows, inner = x.shape
     depth, width = w_ref.shape
     offset = width - inner // depth * slab
     pieces = slab // LANES
+    places = tiles // chips
     for place, w in enumerate((w_ref, other_ref)):
         part = jnp.zeros((rows, slab), WIDE)
         for block in range(inner // depth):
@@ -208,19 +224,26 @@
                 w[:, at : at + slab],
                 preferred_element_type=WIDE,
             )
-        for piece in range(pieces):
-            parts_ref[pl.ds(place * pieces + piece, rows, stride=2 * pieces), :] = part[
-                :, piece * LANES : (piece + 1) * LANES
-            ]
+        for s in range(rows // chips):
+            for piece in range(pieces):
+                line = place * lines + s * pieces + piece
+                parts_ref[pl.ds(line, chips, stride=places * lines), :] = part[
+                    s * chips : (s + 1) * chips, piece * LANES : (piece + 1) * LANES
+                ]
+    for tile in range(tiles):
+        out_ref[tile] = parts_ref[tile * lines : (tile + 1) * lines, :].astype(NARROW)
+
+
+def join(x_ref, out_ref):
+    targets, chips = out_ref.shape[:2]
+    sides = x_ref.shape[0] // chips
     for chip in range(chips):
-        out_ref[chip] = parts_ref[chip * lines : (chip + 1) * lines, :].astype(NARROW)
-
-
-def repeat(x_ref, out_ref):
-    for chip in range(x_ref.shape[0]):
-        x = x_ref[chip]
-        for target in range(out_ref.shape[0]):
-            out_ref[target, chip] = x
+        total = x_ref[chip * sides].astype(WIDE)
+        for side in range(1, sides):
+            total = total + x_ref[chip * sides + side].astype(WIDE)
+        total = total.astype(NARROW)
+        for target in range(targets):
+            out_ref[target, chip] = total
 
 
 def finish(
@@ -229,21 +252,24 @@
     key_ref[...] = key_in[...]
     value_ref[...] = value_in[...]
     core = own_core()
-    chips, lines = parts_ref.shape[1:3]
+    sources, chips, lines = parts_ref.shape[:3]
     sequences = hidden_ref.shape[0]
     pieces = slab // LANES
+    places = 2
     for chip in range(chips):
-        total = parts_ref[0, chip].astype(WIDE)
-        for source in range(1, parts_ref.shape[0]):
-            total = total + parts_ref[source, chip].astype(WIDE)
-        sums_ref[chip * lines : (chip + 1) * lines, :] = total
+        for place in range(places):
+            total = parts_ref[place, chip].astype(WIDE)
+            for source in range(place + places, sources, places):
+                total = total + parts_ref[source, chip].astype(WIDE)
+            tile = chip * places + place
+            sums_ref[tile * lines : (tile + 1) * lines, :] = total
     for chip in range(chips):
-        for place in range(2):
+        for place in range(places):
             index = 2 * chip + (core if place == 0 else 1 - core)
             first = slab_ref[index] * slab
             for piece in range(pieces):
-                line = chip * lines + place * pieces + piece
-                added = sums_ref[pl.ds(line, sequences, stride=lines // sequences), :]
+                line = (chip * places + place) * lines + piece
+                added = sums_ref[pl.ds(line, sequences, stride=pieces), :]
                 at = pl.ds(pl.multiple_of(first + piece * LANES, LANES), LANES)
                 out_ref[:, at] = (hidden_ref[:, at].astype(WIDE) + added).astype(NARROW)
 
@@ -267,6 +293,16 @@
         for core in range(2)
         for pair in range(tensors // 2)
         for side in range(2)
+    ]
+
+    columns_of_x = [
+        [
+            (2 * chip + core) * tensors + pair * 2 + side
+            for chip in range(chips)
+            for side in range(2)
+        ]
+        for core in range(2)
+        for pair in range(tensors // 2)
     ]
 
     def body(
@@ -326,9 +362,10 @@
             heads=heads,
         )
         gathered = exchange(attended, "group", same_core)
+        tile = (lines // 2, LANES)
         head_partial = call(
             project_out,
-            pltpu.VMEM((chips, lines, LANES), NARROW),
+            pltpu.VMEM((2 * chips, *tile), NARROW),
             (),
             (gathered, own_weights, other_weights),
             [
@@ -338,8 +375,8 @@
             heads=heads,
             slab=slab,
         )
-        returned = exchange(head_partial, ("group", "tensor"), near)
-        copies = call(repeat, pltpu.VMEM((tensors, chips, lines, LANES), NARROW), (), (returned,))
+        returned = exchange(head_partial, ("group", "tensor"), columns_of_x)
+        copies = call(join, pltpu.VMEM((tensors, chips, *tile), NARROW), (), (returned,))
         everyone = lax.all_to_all(copies, "tensor", 0, 0, tiled=True)
         out_hidden, new_keys, new_values = call(
             finish,

time: 81.8 us -> 81.5 us (level)
    all_to_all x1, blocking collectives: 14.4 us -> 11.8 us  [body(): everyone = lax.all_to_all(copies, 'tensor', 0, 0, tiled=True)]
    all_to_all x4, blocking collectives: 59.8 us -> 62.2 us  [exchange(): return lax.all_to_all(tiles, axis, 0, 0, tiled=True, axis_index_groups=sets)]
where the time goes in v5:
time: 81.5 us; the launch traced here: 81.2 us
  blocking collectives  74 us (91%)
  Pallas kernels  6.37 us (8%)
    all_to_all x4, blocking collectives, exchange(): return lax.all_to_all(tiles, axis, 0, 0, tiled=True, axis_index_groups=sets)  62.2 us
    all_to_all x1, blocking collectives, body(): everyone = lax.all_to_all(copies, 'tensor', 0, 0, tiled=True)  11.8 us
    pallas_call x6, Pallas kernels, call(): pl.pallas_call(functools.partial(kernel, **sizes), out_shape=outs, in_spe...  6.37 us
  transfers between devices with their start and end apart: 1, of which 0 were waited for; matrix products, arithmetic and copies ran while one was open for 0% of the time, Pallas kernels for 0%

profile of v5, /device:TPU:2, one launch (start us, length us, event | category | flops | bytes accessed | tf_op | source)
XLA Modules:
  0.0 81.2 jit_solution(5277643940679336313)
XLA Ops:
  0.6 2.4 %arrange.1 = (bf16[16,16,128]{2,1,0:T(8,128)(2,1)S(1)}, f32[2,128]{1,0:T(2,128)S(1)}, f32[2,128]{1,0:T(2,128)S(1)}, bf16[512,4352]{1,0:T(8,128)(2,1)S(1)}, s32[2]{0:T(128)S(4)}, /*index=5*/s32[32]{0:T(128)S(4)}) custom-call(s32[2]{0:T(128)} %refs_0_.1, s32[32]{0:T(128)} %refs_1_.1, bf16[2,16384]{1,0:T(2,128)(2,1)} %hidden_ref.1, f32[1,16384]{1,0:T(1,128)} %bitcast.3, ...), custom_call_target="tpu_custom_call" | custom-call | tf_op jit(solution)/shard_map/arrange/pallas_call | solution.py:30
  3.0 0.1 collective-permute-start
  3.1 17.8 %all_to_all.25.x_ref = bf16[16,16,128]{2,1,0:T(8,128)(2,1)S(1)} all-to-all(bf16[16,16,128]{2,1,0:T(8,128)(2,1)S(1)} %get-tuple-element.19), channel_id=1, replica_groups={{0,16,32,48,64,80,96,112,129,145,161,177,193,209,225,241},{1,17,33,49,6..., dimensions={0} | all-to-all | bytes 131072 | tf_op jit(solution)/shard_map/all_to_all | solution.py:278
  21.0 0.0 copy-start
  21.0 0.0 copy-start.1
  21.0 0.0 collective-permute-done.other_ref
  21.0 0.9 %project.1 = f32[16,2,2304]{2,1,0:T(2,128)S(1)} custom-call(bf16[16,16,128]{2,1,0:T(8,128)(2,1)S(1)} %all_to_all.25.x_ref, bf16[512,4352]{1,0:T(8,128)(2,1)S(1)} %get-tuple-element.20.w_ref, bf16[512,4352]{1,0:T(8,128)(2,1)S(1)} %collective-permute-done.other_ref), custom_call_target="tpu_custom_call" | custom-call | tf_op jit(solution)/shard_map/project/pallas_call | solution.py:30
  21.9 16.0 %all_to_all.26.part_ref = f32[16,2,2304]{2,1,0:T(2,128)S(1)} all-to-all(f32[16,2,2304]{2,1,0:T(2,128)S(1)} %project.1), channel_id=1, replica_groups={{0,16,32,48,64,80,96,112,128,144,160,176,192,208,224,240},{8,24,40,56,7..., dimensions={0} | all-to-all | bytes 589824 | tf_op jit(solution)/shard_map/all_to_all | solution.py:278
  37.9 0.0 copy-done
  37.9 0.0 copy-done.1
  37.9 1.4 %attend.1 = (bf16[16,32,128]{2,1,0:T(8,128)(2,1)S(1)}, bf16[2,128]{1,0:T(2,128)(2,1)S(1)}, bf16[2,128]{1,0:T(2,128)(2,1)S(1)}) custom-call(s32[2]{0:T(128)S(4)} %get-tuple-element.18.length_ref, f32[16,2,2304]{2,1,0:T(2,128)S(1)} %all_to_all.26.part_ref, f32[2,128]{1,0:T(2,128)S(1)} %get-tuple-element.23.cos_ref, f32[2,128]{1,0:T(2,128)S(1)} %get-tuple-element.24.sin_ref, ...), custom_call_target="tpu_custom_call" | custom-call | tf_op jit(solution)/shard_map/attend/pallas_call | solution.py:30
  39.3 14.6 %all_to_all.27.x_ref = bf16[16,32,128]{2,1,0:T(8,128)(2,1)S(1)} all-to-all(bf16[16,32,128]{2,1,0:T(8,128)(2,1)S(1)} %get-tuple-element.25), channel_id=1, replica_groups={{0,16,32,48,64,80,96,112,128,144,160,176,192,208,224,240},{8,24,40,56,7..., dimensions={0} | all-to-all | bytes 262144 | tf_op jit(solution)/shard_map/all_to_all | solution.py:278
  53.9 0.0 copy-start.2
  53.9 0.8 %project_out.1 = bf16[32,8,128]{2,1,0:T(8,128)(2,1)S(1)} custom-call(bf16[16,32,128]{2,1,0:T(8,128)(2,1)S(1)} %all_to_all.27.x_ref, bf16[512,4352]{1,0:T(8,128)(2,1)S(1)} %get-tuple-element.20.w_ref, bf16[512,4352]{1,0:T(8,128)(2,1)S(1)} %collective-permute-done.other_ref), custom_call_target="tpu_custom_call" | custom-call | tf_op jit(solution)/shard_map/project_out/pallas_call | solution.py:30
  54.7 13.8 %all_to_all.28.x_ref = bf16[32,8,128]{2,1,0:T(8,128)(2,1)S(1)} all-to-all(bf16[32,8,128]{2,1,0:T(8,128)(2,1)S(1)} %project_out.1), channel_id=1, replica_groups={{0,1,16,17,32,33,48,49,64,65,80,81,96,97,112,113,128,129,144,145,160,16..., dimensions={0} | all-to-all | bytes 131072 | tf_op jit(solution)/shard_map/all_to_all | solution.py:278
  68.5 11.8 %all_to_all.29.parts_ref = bf16[8,16,8,128]{3,2,1,0:T(8,128)(2,1)S(1)} all-to-all(bf16[8,16,8,128]{3,2,1,0:T(8,128)(2,1)S(1)} %join.1), channel_id=1, replica_groups=mesh['group'=32,'tensor'=8] {'tensor'}, dimensions={0} | all-to-all | bytes 524288 | tf_op jit(solution)/shard_map/all_to_all | solution.py:380
  80.4 0.0 copy-done.2
  80.4 0.8 finish.1
  (1 shorter events, 0.0 us)
Async XLA Ops:
  3.0 17.9 %collective-permute-start = (bf16[512,4352]{1,0:T(8,128)(2,1)S(1)}, bf16[512,4352]{1,0:T(8,128)(2,1)S(1)}, u32[]{:S(2)}, u32[]{:S(2)}) collective-permute-start(bf16[512,4352]{1,0:T(8,128)(2,1)S(1)} %get-tuple-element.20.w_ref), channel_id=1, source_target_pairs={{0,8},{8,0},{16,24},{24,16},{32,40},{40,32},{48,56},{56,48},{64,72... | collective-permute-start | bytes 13369352 | tf_op jit(solution)/shard_map/ppermute | solution.py:339
  21.0 16.9 %copy-start = (bf16[2,1,4096,128]{3,2,1,0:T(8,128)(2,1)S(1)}, bf16[2,1,4096,128]{3,2,1,0:T(8,128)(2,1)}, u32[]{:S(2)}) copy-start(bf16[2,1,4096,128]{3,2,1,0:T(8,128)(2,1)} %k_ref.1) | copy-start | bytes 6291460
  21.0 16.9 %copy-start.1 = (bf16[2,1,4096,128]{3,2,1,0:T(8,128)(2,1)S(1)}, bf16[2,1,4096,128]{3,2,1,0:T(8,128)(2,1)}, u32[]{:S(2)}) copy-start(bf16[2,1,4096,128]{3,2,1,0:T(8,128)(2,1)} %v_ref.1) | copy-start | bytes 6291460
  53.9 26.5 %copy-start.2 = (bf16[2,16384]{1,0:T(2,128)(2,1)S(1)}, bf16[2,16384]{1,0:T(2,128)(2,1)}, u32[]{:S(2)}) copy-start(bf16[2,16384]{1,0:T(2,128)(2,1)} %hidden_ref.1) | copy-start | bytes 196612

commit v6 on v5

--- a/solution.py
+++ b/solution.py
@@ -7,6 +7,7 @@
 from jax.experimental import pallas as pl
 from jax.experimental.pallas import tpu as pltpu
 from jax.sharding import PartitionSpec as P
+
 
 ROTARY_BASE = 500000.0
 EPSILON = 1e-05
@@ -39,7 +40,6 @@
         ),
         scratch_shapes=list(scratch),
         compiler_params=pltpu.CompilerParams(vmem_limit_bytes=8 * 1024 * 1024),
-        name=kernel.__name__,
     )(*scalars, *in_hbm(*far), *arrays)
 
 
@@ -48,22 +48,15 @@
 
 
 def arrange(*refs, slab):
-    far, refs = refs[:8], refs[8:]
+    far, refs = refs[:7], refs[7:]
     (
         out_ref, cos_ref, sin_ref, kept_ref, length_ref, slab_ref, hidden_ref, gain_ref, rows_ref, sems
     ) = refs
     near = [length_ref, slab_ref, hidden_ref, gain_ref]
-    far = list(far)
     offset = 0
-    w_out = far.pop()
     for weight in far[4:]:
         near.append(kept_ref.at[:, offset : offset + weight.shape[1]])
         offset += weight.shape[1]
-    depth, columns = kept_ref.shape[0], w_out.shape[1]
-    for first in range(0, w_out.shape[0], depth):
-        far.append(w_out.at[first : first + depth, :])
-        near.append(kept_ref.at[:, offset : offset + columns])
-        offset += columns
     copies = [pltpu.make_async_copy(f, n, sems.at[i]) for i, (f, n) in enumerate(zip(far, near))]
     for copy in copies:
         copy.start()
@@ -206,24 +199,15 @@
             out_ref[target, s * heads : (s + 1) * heads, :] = attended
 
 
-def project_out(x_ref, w_ref, other_ref, out_ref, rows_ref, parts_ref, *, heads, slab):
+def project_out(x_ref, w_ref, other_ref, out_ref, rows_ref, parts_ref, *, heads):
     chips = x_ref.shape[0]
     tiles, lines = out_ref.shape[:2]
     x = rows_of(x_ref, rows_ref, heads, by_sequence=True)
-    rows, inner = x.shape
-    depth, width = w_ref.shape
-    offset = width - inner // depth * slab
+    rows, slab = x.shape[0], w_ref.shape[1]
     pieces = slab // LANES
     places = tiles // chips
     for place, w in enumerate((w_ref, other_ref)):
-        part = jnp.zeros((rows, slab), WIDE)
-        for block in range(inner // depth):
-            at = offset + block * slab
-            part += jnp.dot(
-                x[:, block * depth : (block + 1) * depth],
-                w[:, at : at + slab],
-                preferred_element_type=WIDE,
-            )
+        part = jnp.dot(x, w[...], preferred_element_type=WIDE)
         for s in range(rows // chips):
             for piece in range(pieces):
                 line = place * lines + s * pieces + piece
@@ -314,14 +298,14 @@
         heads = w_query.shape[1] // head_dim
         columns = w_query.shape[1] + w_key.shape[1] + w_value.shape[1]
         lines = sequences * 2 * slab // LANES
-        kept = columns + w_out.shape[0] // slab * slab
+        other_out = lax.ppermute(w_out, "group", partner)
         arranged, cosine, sine, own_weights, near_lengths, near_slabs = call(
             arrange,
             (
                 pltpu.VMEM((chips, lines, LANES), NARROW),
                 pltpu.VMEM((sequences, head_dim), WIDE),
                 pltpu.VMEM((sequences, head_dim), WIDE),
-                pltpu.VMEM((slab, kept), NARROW),
+                pltpu.VMEM((slab, columns), NARROW),
                 pltpu.SMEM((sequences,), jnp.int32),
                 pltpu.SMEM((groups,), jnp.int32),
             ),
@@ -331,14 +315,16 @@
                 pltpu.VMEM((sequences, width), NARROW),
                 pltpu.VMEM((1, width), WIDE),
                 pltpu.VMEM((chips * lines, LANES), WIDE),
-                pltpu.SemaphoreType.DMA((7 + w_out.shape[0] // slab,)),
+                pltpu.SemaphoreType.DMA((7,)),
             ],
-            (lengths, slab_of, hidden, norm_gain.reshape(1, width), w_query, w_key, w_value, w_out),
+            (lengths, slab_of, hidden, norm_gain.reshape(1, width), w_query, w_key, w_value),
             slab=slab,
         )
         other_weights = lax.ppermute(own_weights, "group", partner)
         features = exchange(arranged, ("group", "tensor"), near)
-        features, other_weights = lax.optimization_barrier((features, other_weights))
+        features, other_weights, other_out = lax.optimization_barrier(
+            (features, other_weights, other_out)
+        )
         other_weights, = in_vmem(other_weights)
         partial = call(
             project,
@@ -349,6 +335,7 @@
             chunk=512,
         )
         parts = exchange(partial, "group", same_core)
+        parts, own_out = lax.optimization_barrier((parts, w_out))
         attended, new_keys, new_values = call(
             attend,
             (
@@ -367,13 +354,12 @@
             project_out,
             pltpu.VMEM((2 * chips, *tile), NARROW),
             (),
-            (gathered, own_weights, other_weights),
+            (gathered, *in_vmem(own_out, other_out)),
             [
                 pltpu.VMEM((chips * sequences * heads, head_dim), WIDE),
                 pltpu.VMEM((chips * lines, LANES), WIDE),
             ],
             heads=heads,
-            slab=slab,
         )
         returned = exchange(head_partial, ("group", "tensor"), columns_of_x)
         copies = call(join, pltpu.VMEM((tensors, chips, *tile), NARROW), (), (returned,))

time: 81.5 us -> 81.3 us (level)
  transfers between devices with their start and end apart: 1 -> 2, of which waited for: 0 -> 0; matrix products, arithmetic and copies ran while one was open for 0% -> 0% of each run, Pallas kernels for 0% -> 0%
where the time goes in v6:
time: 81.3 us; the launch traced here: 81.1 us
  blocking collectives  73.9 us (91%)
  Pallas kernels  5.84 us (7%)
    all_to_all x4, blocking collectives, exchange(): return lax.all_to_all(tiles, axis, 0, 0, tiled=True, axis_index_groups=sets)  62.1 us
    all_to_all x1, blocking collectives, body(): everyone = lax.all_to_all(copies, 'tensor', 0, 0, tiled=True)  11.8 us
    pallas_call x6, Pallas kernels, call(): pl.pallas_call(functools.partial(kernel, **sizes), out_shape=outs, in_spe...  5.84 us
  transfers between devices with their start and end apart: 2, of which 0 were waited for; matrix products, arithmetic and copies ran while one was open for 0% of the time, Pallas kernels for 0%

profile of v6, /device:TPU:2, one launch (start us, length us, event | category | flops | bytes accessed | tf_op | source)
XLA Modules:
  0.0 81.1 jit_solution(484786073134484246)
XLA Ops:
  0.6 0.0 copy-start.2
  0.6 1.9 %shard_map.121 = (bf16[16,16,128]{2,1,0:T(8,128)(2,1)S(1)}, f32[2,128]{1,0:T(2,128)S(1)}, f32[2,128]{1,0:T(2,128)S(1)}, bf16[512,2304]{1,0:T(8,128)(2,1)S(1)}, s32[2]{0:T(128)S(4)}, /*index=5*/s32[32]{0:T(128)S(4)}) custom-call(s32[2]{0:T(128)} %refs_0_.1, s32[32]{0:T(128)} %refs_1_.1, bf16[2,16384]{1,0:T(2,128)(2,1)} %hidden_ref.1, f32[1,16384]{1,0:T(1,128)} %bitcast.3, ...), custom_call_target="tpu_custom_call" | custom-call | tf_op jit(solution)/shard_map/pallas_call | solution.py:31
  2.5 0.1 collective-permute-start
  2.6 0.4 copy-done.2
  3.0 0.1 collective-permute-start.1
  3.1 17.8 %all_to_all.25.x_ref = bf16[16,16,128]{2,1,0:T(8,128)(2,1)S(1)} all-to-all(bf16[16,16,128]{2,1,0:T(8,128)(2,1)S(1)} %get-tuple-element.22), channel_id=1, replica_groups={{0,16,32,48,64,80,96,112,129,145,161,177,193,209,225,241},{1,17,33,49,6..., dimensions={0} | all-to-all | bytes 131072 | tf_op jit(solution)/shard_map/all_to_all | solution.py:262
  20.9 0.0 copy-start
  20.9 0.0 copy-start.1
  20.9 0.0 collective-permute-done.1.other_ref
  20.9 0.0 collective-permute-done.other_ref
  20.9 0.9 %shard_map.122 = f32[16,2,2304]{2,1,0:T(2,128)S(1)} custom-call(bf16[16,16,128]{2,1,0:T(8,128)(2,1)S(1)} %all_to_all.25.x_ref, bf16[512,2304]{1,0:T(8,128)(2,1)S(1)} %get-tuple-element.23.w_ref, bf16[512,2304]{1,0:T(8,128)(2,1)S(1)} %collective-permute-done.other_ref), custom_call_target="tpu_custom_call" | custom-call | tf_op jit(solution)/shard_map/pallas_call | solution.py:31
  21.9 15.9 %all_to_all.26.part_ref = f32[16,2,2304]{2,1,0:T(2,128)S(1)} all-to-all(f32[16,2,2304]{2,1,0:T(2,128)S(1)} %shard_map.122), channel_id=1, replica_groups={{0,16,32,48,64,80,96,112,128,144,160,176,192,208,224,240},{8,24,40,56,7..., dimensions={0} | all-to-all | bytes 589824 | tf_op jit(solution)/shard_map/all_to_all | solution.py:262
  37.7 0.0 copy-done
  37.8 0.0 copy-done.1
  37.8 1.4 %shard_map.123 = (bf16[16,32,128]{2,1,0:T(8,128)(2,1)S(1)}, bf16[2,128]{1,0:T(2,128)(2,1)S(1)}, bf16[2,128]{1,0:T(2,128)(2,1)S(1)}) custom-call(s32[2]{0:T(128)S(4)} %get-tuple-element.21.length_ref, f32[16,2,2304]{2,1,0:T(2,128)S(1)} %all_to_all.26.part_ref, f32[2,128]{1,0:T(2,128)S(1)} %get-tuple-element.27.cos_ref, ...), custom_call_target="tpu_custom_call" | custom-call | tf_op jit(solution)/shard_map/pallas_call | solution.py:31
  39.2 14.6 %all_to_all.27.x_ref = bf16[16,32,128]{2,1,0:T(8,128)(2,1)S(1)} all-to-all(bf16[16,32,128]{2,1,0:T(8,128)(2,1)S(1)} %get-tuple-element.29), channel_id=1, replica_groups={{0,16,32,48,64,80,96,112,128,144,160,176,192,208,224,240},{8,24,40,56,7..., dimensions={0} | all-to-all | bytes 262144 | tf_op jit(solution)/shard_map/all_to_all | solution.py:262
  53.8 0.0 copy-start.3
  53.8 0.8 shard_map.124
  54.6 13.8 %all_to_all.28.x_ref = bf16[32,8,128]{2,1,0:T(8,128)(2,1)S(1)} all-to-all(bf16[32,8,128]{2,1,0:T(8,128)(2,1)S(1)} %shard_map.124), channel_id=1, replica_groups={{0,1,16,17,32,33,48,49,64,65,80,81,96,97,112,113,128,129,144,145,160,16..., dimensions={0} | all-to-all | bytes 131072 | tf_op jit(solution)/shard_map/all_to_all | solution.py:262
  68.4 11.8 %all_to_all.29.parts_ref = bf16[8,16,8,128]{3,2,1,0:T(8,128)(2,1)S(1)} all-to-all(bf16[8,16,8,128]{3,2,1,0:T(8,128)(2,1)S(1)} %shard_map.125), channel_id=1, replica_groups=mesh['group'=32,'tensor'=8] {'tensor'}, dimensions={0} | all-to-all | bytes 524288 | tf_op jit(solution)/shard_map/all_to_all | solution.py:366
  80.3 0.0 copy-done.3
  80.3 0.8 shard_map.126
  (1 shorter events, 0.0 us)
Async XLA Ops:
  0.6 2.4 %copy-start.2 = (bf16[2048,512]{1,0:T(8,128)(2,1)S(1)}, bf16[2048,512]{1,0:T(8,128)(2,1)}, u32[]{:S(2)}) copy-start(bf16[2048,512]{1,0:T(8,128)(2,1)} %w_ref) | copy-start | bytes 6291460
  2.5 18.4 %collective-permute-start = (bf16[512,2304]{1,0:T(8,128)(2,1)S(1)}, bf16[512,2304]{1,0:T(8,128)(2,1)S(1)}, u32[]{:S(2)}, u32[]{:S(2)}) collective-permute-start(bf16[512,2304]{1,0:T(8,128)(2,1)S(1)} %get-tuple-element.23.w_ref), channel_id=1, source_target_pairs={{0,8},{8,0},{16,24},{24,16},{32,40},{40,32},{48,56},{56,48},{64,72... | collective-permute-start | bytes 7077896 | tf_op jit(solution)/shard_map/ppermute | solution.py:323
  3.0 17.9 %collective-permute-start.1 = (bf16[2048,512]{1,0:T(8,128)(2,1)S(1)}, bf16[2048,512]{1,0:T(8,128)(2,1)S(1)}, u32[]{:S(2)}, u32[]{:S(2)}) collective-permute-start(bf16[2048,512]{1,0:T(8,128)(2,1)S(1)} %copy-done.2), channel_id=1, source_target_pairs={{0,8},{8,0},{16,24},{24,16},{32,40},{40,32},{48,56},{56,48},{64,72... | collective-permute-start | bytes 6291464 | tf_op jit(solution)/shard_map/ppermute | solution.py:301
  20.9 16.8 %copy-start = (bf16[2,1,4096,128]{3,2,1,0:T(8,128)(2,1)S(1)}, bf16[2,1,4096,128]{3,2,1,0:T(8,128)(2,1)}, u32[]{:S(2)}) copy-start(bf16[2,1,4096,128]{3,2,1,0:T(8,128)(2,1)} %k_ref.1) | copy-start | bytes 6291460
  20.9 16.8 %copy-start.1 = (bf16[2,1,4096,128]{3,2,1,0:T(8,128)(2,1)S(1)}, bf16[2,1,4096,128]{3,2,1,0:T(8,128)(2,1)}, u32[]{:S(2)}) copy-start(bf16[2,1,4096,128]{3,2,1,0:T(8,128)(2,1)} %v_ref.1) | copy-start | bytes 6291460
  53.8 26.5 %copy-start.3 = (bf16[2,16384]{1,0:T(2,128)(2,1)S(1)}, bf16[2,16384]{1,0:T(2,128)(2,1)}, u32[]{:S(2)}) copy-start(bf16[2,16384]{1,0:T(2,128)(2,1)} %hidden_ref.1) | copy-start | bytes 196612

commit v7 on v6

--- a/solution.py
+++ b/solution.py
@@ -174,22 +174,35 @@
         ],
         axis=0,
     )
-    keys = jnp.concatenate([k_ref[s, 0] for s in range(sequences)], axis=1)
-    scores = lax.dot_general(
-        queries, keys, (((1,), (1,)), ((), ())), preferred_element_type=WIDE
-    )
-    weights, own_weights = [], []
+    step = cached // 4
+    masked, highest = [], [own for own in own_scores]
+    for first in range(0, cached, step):
+        keys = jnp.concatenate([k_ref[s, 0, first : first + step, :] for s in range(sequences)], axis=1)
+        scores = lax.dot_general(
+            queries, keys, (((1,), (1,)), ((), ())), preferred_element_type=WIDE
+        )
+        for s in range(sequences):
+            slot = lax.broadcasted_iota(jnp.int32, (heads, step), 1) + first
+            seen = jnp.where(slot < length_ref[s], scores[s * heads : (s + 1) * heads], -1e30)
+            masked.append(seen)
+            highest[s] = jnp.maximum(highest[s], jnp.max(seen, axis=1, keepdims=True))
+    exponents, shares, own_weights = [None] * len(masked), [], []
     for s in range(sequences):
-        visible = lax.broadcasted_iota(jnp.int32, (heads, cached), 1) < length_ref[s]
-        masked = jnp.where(visible, scores[s * heads : (s + 1) * heads], -1e30)
-        highest = jnp.maximum(jnp.max(masked, axis=1, keepdims=True), own_scores[s])
-        exponent = jnp.exp(masked - highest)
-        own_exp = jnp.exp(own_scores[s] - highest)
-        share = 1.0 / (jnp.sum(exponent, axis=1, keepdims=True) + own_exp)
-        weights.append((exponent * share).astype(NARROW))
-        own_weights.append((own_exp * share).astype(NARROW))
-    values = jnp.concatenate([v_ref[s, 0] for s in range(sequences)], axis=1)
-    combined = jnp.dot(jnp.concatenate(weights, axis=0), values, preferred_element_type=WIDE)
+        own_exp = jnp.exp(own_scores[s] - highest[s])
+        total_exp = own_exp
+        for i in range(s, len(masked), sequences):
+            exponents[i] = jnp.exp(masked[i] - highest[s])
+            total_exp = total_exp + jnp.sum(exponents[i], axis=1, keepdims=True)
+        shares.append(1.0 / total_exp)
+        own_weights.append((own_exp * shares[s]).astype(NARROW))
+    combined = jnp.zeros((sequences * heads, sequences * head_dim), WIDE)
+    for i in range(0, len(masked), sequences):
+        first = i // sequences * step
+        weights = jnp.concatenate(
+            [(exponents[i + s] * shares[s]).astype(NARROW) for s in range(sequences)], axis=0
+        )
+        values = jnp.concatenate([v_ref[s, 0, first : first + step, :] for s in range(sequences)], axis=1)
+        combined = combined + jnp.dot(weights, values, preferred_element_type=WIDE)
     for s in range(sequences):
         new_value = heads_ref[s, heads + 1 : heads + 2, :].astype(NARROW)
         mixed = combined[s * heads : (s + 1) * heads, s * head_dim : (s + 1) * head_dim]
@@ -332,7 +345,7 @@
             (),
             (features, own_weights, other_weights),
             [pltpu.VMEM((chips * lines, LANES), WIDE)],
-            chunk=512,
+            chunk=1024,
         )
         parts = exchange(partial, "group", same_core)
         parts, own_out = lax.optimization_barrier((parts, w_out))

time: 81.3 us -> 81.3 us (level)
  no operation moved by 1% of the time
where the time goes in v7:
time: 81.3 us; the launch traced here: 81.1 us
  blocking collectives  73.9 us (91%)
  Pallas kernels  5.84 us (7%)
    all_to_all x4, blocking collectives, exchange(): return lax.all_to_all(tiles, axis, 0, 0, tiled=True, axis_index_groups=sets)  62.1 us
    all_to_all x1, blocking collectives, body(): everyone = lax.all_to_all(copies, 'tensor', 0, 0, tiled=True)  11.8 us
    pallas_call x6, Pallas kernels, call(): pl.pallas_call(functools.partial(kernel, **sizes), out_shape=outs, in_spe...  5.84 us
  transfers between devices with their start and end apart: 2, of which 0 were waited for; matrix products, arithmetic and copies ran while one was open for 0% of the time, Pallas kernels for 0%

profile of v7, /device:TPU:2, one launch (start us, length us, event | category | flops | bytes accessed | tf_op | source)
XLA Modules:
  0.0 81.1 jit_solution(4937576372837770945)
XLA Ops:
  0.6 0.0 copy-start.2
  0.6 1.9 %shard_map.121 = (bf16[16,16,128]{2,1,0:T(8,128)(2,1)S(1)}, f32[2,128]{1,0:T(2,128)S(1)}, f32[2,128]{1,0:T(2,128)S(1)}, bf16[512,2304]{1,0:T(8,128)(2,1)S(1)}, s32[2]{0:T(128)S(4)}, /*index=5*/s32[32]{0:T(128)S(4)}) custom-call(s32[2]{0:T(128)} %refs_0_.1, s32[32]{0:T(128)} %refs_1_.1, bf16[2,16384]{1,0:T(2,128)(2,1)} %hidden_ref.1, f32[1,16384]{1,0:T(1,128)} %bitcast.3, ...), custom_call_target="tpu_custom_call" | custom-call | tf_op jit(solution)/shard_map/pallas_call | solution.py:31
  2.5 0.1 collective-permute-start
  2.6 0.4 copy-done.2
  3.0 0.1 collective-permute-start.1
  3.1 17.8 %all_to_all.25.x_ref = bf16[16,16,128]{2,1,0:T(8,128)(2,1)S(1)} all-to-all(bf16[16,16,128]{2,1,0:T(8,128)(2,1)S(1)} %get-tuple-element.22), channel_id=1, replica_groups={{0,16,32,48,64,80,96,112,129,145,161,177,193,209,225,241},{1,17,33,49,6..., dimensions={0} | all-to-all | bytes 131072 | tf_op jit(solution)/shard_map/all_to_all | solution.py:275
  20.9 0.0 copy-start
  20.9 0.0 copy-start.1
  20.9 0.0 collective-permute-done.1.other_ref
  20.9 0.0 collective-permute-done.other_ref
  20.9 0.9 %shard_map.122 = f32[16,2,2304]{2,1,0:T(2,128)S(1)} custom-call(bf16[16,16,128]{2,1,0:T(8,128)(2,1)S(1)} %all_to_all.25.x_ref, bf16[512,2304]{1,0:T(8,128)(2,1)S(1)} %get-tuple-element.23.w_ref, bf16[512,2304]{1,0:T(8,128)(2,1)S(1)} %collective-permute-done.other_ref), custom_call_target="tpu_custom_call" | custom-call | tf_op jit(solution)/shard_map/pallas_call | solution.py:31
  21.9 15.9 %all_to_all.26.part_ref = f32[16,2,2304]{2,1,0:T(2,128)S(1)} all-to-all(f32[16,2,2304]{2,1,0:T(2,128)S(1)} %shard_map.122), channel_id=1, replica_groups={{0,16,32,48,64,80,96,112,128,144,160,176,192,208,224,240},{8,24,40,56,7..., dimensions={0} | all-to-all | bytes 589824 | tf_op jit(solution)/shard_map/all_to_all | solution.py:275
  37.8 0.0 copy-done
  37.8 0.0 copy-done.1
  37.8 1.4 %shard_map.123 = (bf16[16,32,128]{2,1,0:T(8,128)(2,1)S(1)}, bf16[2,128]{1,0:T(2,128)(2,1)S(1)}, bf16[2,128]{1,0:T(2,128)(2,1)S(1)}) custom-call(s32[2]{0:T(128)S(4)} %get-tuple-element.21.length_ref, f32[16,2,2304]{2,1,0:T(2,128)S(1)} %all_to_all.26.part_ref, f32[2,128]{1,0:T(2,128)S(1)} %get-tuple-element.27.cos_ref, ...), custom_call_target="tpu_custom_call" | custom-call | tf_op jit(solution)/shard_map/pallas_call | solution.py:31
  39.2 14.6 %all_to_all.27.x_ref = bf16[16,32,128]{2,1,0:T(8,128)(2,1)S(1)} all-to-all(bf16[16,32,128]{2,1,0:T(8,128)(2,1)S(1)} %get-tuple-element.29), channel_id=1, replica_groups={{0,16,32,48,64,80,96,112,128,144,160,176,192,208,224,240},{8,24,40,56,7..., dimensions={0} | all-to-all | bytes 262144 | tf_op jit(solution)/shard_map/all_to_all | solution.py:275
  53.8 0.0 copy-start.3
  53.8 0.8 shard_map.124
  54.6 13.8 %all_to_all.28.x_ref = bf16[32,8,128]{2,1,0:T(8,128)(2,1)S(1)} all-to-all(bf16[32,8,128]{2,1,0:T(8,128)(2,1)S(1)} %shard_map.124), channel_id=1, replica_groups={{0,1,16,17,32,33,48,49,64,65,80,81,96,97,112,113,128,129,144,145,160,16..., dimensions={0} | all-to-all | bytes 131072 | tf_op jit(solution)/shard_map/all_to_all | solution.py:275
  68.4 11.8 %all_to_all.29.parts_ref = bf16[8,16,8,128]{3,2,1,0:T(8,128)(2,1)S(1)} all-to-all(bf16[8,16,8,128]{3,2,1,0:T(8,128)(2,1)S(1)} %shard_map.125), channel_id=1, replica_groups=mesh['group'=32,'tensor'=8] {'tensor'}, dimensions={0} | all-to-all | bytes 524288 | tf_op jit(solution)/shard_map/all_to_all | solution.py:379
  80.3 0.0 copy-done.3
  80.3 0.8 shard_map.126
  (1 shorter events, 0.0 us)
Async XLA Ops:
  0.6 2.4 %copy-start.2 = (bf16[2048,512]{1,0:T(8,128)(2,1)S(1)}, bf16[2048,512]{1,0:T(8,128)(2,1)}, u32[]{:S(2)}) copy-start(bf16[2048,512]{1,0:T(8,128)(2,1)} %w_ref) | copy-start | bytes 6291460
  2.5 18.4 %collective-permute-start = (bf16[512,2304]{1,0:T(8,128)(2,1)S(1)}, bf16[512,2304]{1,0:T(8,128)(2,1)S(1)}, u32[]{:S(2)}, u32[]{:S(2)}) collective-permute-start(bf16[512,2304]{1,0:T(8,128)(2,1)S(1)} %get-tuple-element.23.w_ref), channel_id=1, source_target_pairs={{0,8},{8,0},{16,24},{24,16},{32,40},{40,32},{48,56},{56,48},{64,72... | collective-permute-start | bytes 7077896 | tf_op jit(solution)/shard_map/ppermute | solution.py:336
  3.0 17.9 %collective-permute-start.1 = (bf16[2048,512]{1,0:T(8,128)(2,1)S(1)}, bf16[2048,512]{1,0:T(8,128)(2,1)S(1)}, u32[]{:S(2)}, u32[]{:S(2)}) collective-permute-start(bf16[2048,512]{1,0:T(8,128)(2,1)S(1)} %copy-done.2), channel_id=1, source_target_pairs={{0,8},{8,0},{16,24},{24,16},{32,40},{40,32},{48,56},{56,48},{64,72... | collective-permute-start | bytes 6291464 | tf_op jit(solution)/shard_map/ppermute | solution.py:314
  20.9 16.8 %copy-start = (bf16[2,1,4096,128]{3,2,1,0:T(8,128)(2,1)S(1)}, bf16[2,1,4096,128]{3,2,1,0:T(8,128)(2,1)}, u32[]{:S(2)}) copy-start(bf16[2,1,4096,128]{3,2,1,0:T(8,128)(2,1)} %k_ref.1) | copy-start | bytes 6291460
  20.9 16.8 %copy-start.1 = (bf16[2,1,4096,128]{3,2,1,0:T(8,128)(2,1)S(1)}, bf16[2,1,4096,128]{3,2,1,0:T(8,128)(2,1)}, u32[]{:S(2)}) copy-start(bf16[2,1,4096,128]{3,2,1,0:T(8,128)(2,1)} %v_ref.1) | copy-start | bytes 6291460
  53.8 26.5 %copy-start.3 = (bf16[2,16384]{1,0:T(2,128)(2,1)S(1)}, bf16[2,16384]{1,0:T(2,128)(2,1)}, u32[]{:S(2)}) copy-start(bf16[2,16384]{1,0:T(2,128)(2,1)} %hidden_ref.1) | copy-start | bytes 196612
